TPU v7x, 32 devices: a whole 2x2x4 slice. The times are simulated.
32 devices in a mesh: dp: 8 (over z, y), mp: 4 (over x, core).
Axes of the slice: x: 2, y: 2, z: 4, core: 2. Of those that a mesh axis runs over, the one named last changes fastest.
Arguments:
- block_input: bfloat16 [16, 1024, 1536], P('dp'), may hold values from -6 to 6
- zx_weight: bfloat16 [2, 2, 1536, 3072], P(None, None, 'dp', 'mp'), may hold values from -0.15625 to 0.15625
- bc_weight: bfloat16 [2, 1536, 256], P(None, 'dp'), may hold values from -0.15625 to 0.15625
- dt_weight: bfloat16 [2, 1536, 48], P(None, 'dp', 'mp'), may hold values from -0.15625 to 0.15625
- out_weight: bfloat16 [2, 3072, 1536], P(None, 'mp', 'dp'), may hold values from -0.109375 to 0.109375
- norm_gain: float32 [2, 1536], replicated, may hold values from 0.1 to 1.9
- inner_conv: float32 [2, 4, 3072], P(None, None, 'mp'), may hold values from -3 to 3
- inner_conv_bias: float32 [2, 3072], P(None, 'mp'), may hold values from -3 to 3
- state_conv: float32 [2, 4, 256], replicated, may hold values from -3 to 3
- state_conv_bias: float32 [2, 256], replicated, may hold values from -3 to 3
- dt_bias: float32 [2, 48], P(None, 'mp'), may hold values from -5 to -1
- a_log: float32 [2, 48], P(None, 'mp'), may hold values from 0 to 2.5
- d_skip: float32 [2, 48], P(None, 'mp'), may hold values from 0.5 to 2
- gated_gain: float32 [2, 3072], P(None, 'mp'), may hold values from 0.1 to 1.9
- cotangent: bfloat16 [16, 1024, 1536], P('dp'), may hold values from -6 to 6
Outputs:
- block_output: bfloat16 [16, 1024, 1536], P('dp')
- input_grad: float32 [16, 1024, 1536], P('dp')
- zx_grad: float32 [2, 2, 1536, 3072], P(None, None, 'dp', 'mp')
- bc_grad: float32 [2, 1536, 256], P(None, 'dp')
- dt_grad: float32 [2, 1536, 48], P(None, 'dp', 'mp')
- out_grad: float32 [2, 3072, 1536], P(None, 'mp', 'dp')
- norm_gain_grad: float32 [2, 1536], replicated
- inner_conv_grad: float32 [2, 4, 3072], P(None, None, 'mp')
- inner_conv_bias_grad: float32 [2, 3072], P(None, 'mp')
- state_conv_grad: float32 [2, 4, 256], replicated
- state_conv_bias_grad: float32 [2, 256], replicated
- dt_bias_grad: float32 [2, 48], P(None, 'mp')
- a_log_grad: float32 [2, 48], P(None, 'mp')
- d_skip_grad: float32 [2, 48], P(None, 'mp')
- gated_gain_grad: float32 [2, 3072], P(None, 'mp')
All inputs are finite; a program needn't handle non-finite values.
Results may differ from a plain program's by a relative error of at most 0.035.
Values may be sent and summed in bfloat16 or wider, within the bound.
A program may use at most 320 MiB of HBM per device.

v0:
```python
import jax
import jax.numpy as jnp
from jax import lax
from jax.sharding import PartitionSpec as P

SCAN_BLOCK = 256


EPS = 1e-05
HIGH = lax.Precision.HIGHEST


def causal_conv(values, kernel, offset):
    length = values.shape[0]
    taps = kernel.shape[0]
    padded = jnp.pad(values, ((taps - 1, 0), (0, 0)))
    running = jnp.zeros_like(values) + offset[None, :]
    for tap_at in range(taps):
        running = running + kernel[tap_at][None, :] * padded[tap_at : tap_at + length]
    return running


def block_scan(inner_flat, head_count, step_vals, decay_rates, key_rows, query_rows, block_len):
    length, inner_width = inner_flat.shape
    head_width = inner_width // head_count
    block_count = length // block_len
    state_size = key_rows.shape[1]
    inner_blocks = inner_flat.reshape(block_count, block_len, inner_width)
    step_blocks = step_vals.reshape(block_count, block_len, head_count)
    key_blocks = key_rows.reshape(block_count, block_len, state_size)
    query_blocks = query_rows.reshape(block_count, block_len, state_size)
    lower_mask = jnp.tril(jnp.ones((block_len, block_len), jnp.float32))[:, :, None]

    def one_block(carried, pieces):
        flat_values, deltas, keys_here, queries_here = pieces
        values = flat_values.reshape(block_len, head_count, head_width)
        log_decay = jnp.cumsum(deltas * decay_rates[None, :], axis=0)
        scores = jnp.dot(queries_here, keys_here.T, precision=HIGH)
        gaps = log_decay[:, None, :] - log_decay[None, :, :]
        decays = lower_mask * jnp.exp(jnp.where(lower_mask > 0, gaps, 0.0))
        mixing = scores[:, :, None] * decays * deltas[None, :, :]
        within = jnp.einsum("tsh,shp->thp", mixing, values, precision=HIGH)
        from_state = jnp.exp(log_decay)[:, :, None] * jnp.einsum(
            "tn,hpn->thp", queries_here, carried, precision=HIGH
        )
        final_log = log_decay[-1]
        weights_end = jnp.exp(final_log[None, :] - log_decay) * deltas
        update = jnp.einsum("sh,shp,sn->hpn", weights_end, values, keys_here, precision=HIGH)
        return (
            jnp.exp(final_log)[:, None, None] * carried + update,
            (within + from_state).reshape(block_len, inner_width),
        )

    start = jnp.zeros((head_count, head_width, state_size), jnp.float32)
    ended, outputs = lax.scan(
        jax.checkpoint(one_block), start, (inner_blocks, step_blocks, key_blocks, query_blocks)
    )
    return outputs.reshape(length, inner_width)


def ssd_mixer(
    gate_part,
    inner_part,
    state_part,
    step_raw,
    inner_conv,
    inner_conv_bias,
    state_conv,
    state_conv_bias,
    dt_bias,
    a_log,
    d_skip,
):
    head_count = dt_bias.shape[0]
    inner_act = jax.nn.silu(causal_conv(inner_part, inner_conv, inner_conv_bias))
    state_act = jax.nn.silu(causal_conv(state_part, state_conv, state_conv_bias))
    half_state = state_act.shape[1] // 2
    step_pos = jax.nn.softplus(step_raw + dt_bias[None, :])
    decay_rates = -jnp.exp(a_log)
    head_width = inner_act.shape[1] // head_count
    scanned = block_scan(
        inner_act,
        head_count,
        step_pos,
        decay_rates,
        state_act[:, :half_state],
        state_act[:, half_state:],
        SCAN_BLOCK,
    )
    skip_cols = jnp.repeat(d_skip, head_width)
    mixed_out = scanned + skip_cols[None, :] * inner_act
    return mixed_out * jax.nn.silu(gate_part)


def gather_layer(zx_weight, bc_weight, dt_weight, out_weight, layer_at):
    return (
        lax.all_gather(zx_weight[layer_at], "dp", axis=1, tiled=True),
        lax.all_gather(bc_weight[layer_at], "dp", axis=0, tiled=True),
        lax.all_gather(dt_weight[layer_at], "dp", axis=0, tiled=True),
        lax.all_gather(out_weight[layer_at], "dp", axis=1, tiled=True),
    )


def per_device(
    block_input,
    zx_weight,
    bc_weight,
    dt_weight,
    out_weight,
    norm_gain,
    inner_conv,
    inner_conv_bias,
    state_conv,
    state_conv_bias,
    dt_bias,
    a_log,
    d_skip,
    gated_gain,
    cotangent,
):
    layers = zx_weight.shape[0]
    smalls = (
        norm_gain,
        inner_conv,
        inner_conv_bias,
        state_conv,
        state_conv_bias,
        dt_bias,
        a_log,
        d_skip,
        gated_gain,
    )
    inner_total = gated_gain.shape[1] * lax.axis_size("mp")
    model_width = norm_gain.shape[1]
    local_inner = zx_weight.shape[3]
    pair_width = bc_weight.shape[2]
    local_heads = dt_weight.shape[2]

    def fetch_layer(layer_at):
        return gather_layer(zx_weight, bc_weight, dt_weight, out_weight, layer_at)

    big_shapes = (
        (2, model_width, local_inner),
        (model_width, pair_width),
        (model_width, local_heads),
        (local_inner, model_width),
    )
    big_init = tuple(
        (
            tuple((jnp.zeros(shape_of, jnp.float32) for shape_of in big_shapes))
            for layer_at in range(layers)
        )
    )
    small_init = tuple(
        (
            tuple((jnp.zeros(item.shape[1:], jnp.float32) for item in smalls))
            for layer_at in range(layers)
        )
    )

    def micro_step(carried_sums, pair_in):
        big_acc, small_acc = carried_sums
        sequence, tangent = pair_in
        hidden = sequence.astype(jnp.float32)
        records = []
        for layer_at in range(layers):
            gathered = fetch_layer(layer_at)
            zx_full, bc_full, dt_full, out_full = gathered
            params = tuple((item[layer_at] for item in smalls))
            root_row = lax.rsqrt(jnp.mean(hidden * hidden, axis=-1) + EPS)
            normed = (hidden * root_row[:, None] * params[0][None, :]).astype(jnp.bfloat16)
            both_parts = jnp.einsum(
                "td,kdi->tki", normed, zx_full, preferred_element_type=jnp.float32
            )
            state_part = jnp.dot(normed, bc_full, preferred_element_type=jnp.float32)
            step_raw = jnp.dot(normed, dt_full, preferred_element_type=jnp.float32)
            gated_val, pullback = jax.vjp(
                ssd_mixer,
                both_parts[:, 0],
                both_parts[:, 1],
                state_part,
                step_raw,
                params[1],
                params[2],
                params[3],
                params[4],
                params[5],
                params[6],
                params[7],
            )
            squares = lax.psum(jnp.sum(gated_val * gated_val, axis=-1), "mp")
            scale_row = lax.rsqrt(squares / inner_total + EPS)
            weighted = (gated_val * params[8][None, :]).astype(jnp.bfloat16)
            partial_out = jnp.dot(weighted, out_full, preferred_element_type=jnp.float32).astype(
                jnp.bfloat16
            )
            summed = lax.psum(partial_out, "mp").astype(jnp.float32)
            records.append(
                (
                    hidden,
                    root_row,
                    normed,
                    gathered,
                    pullback,
                    gated_val,
                    scale_row,
                    weighted,
                    summed,
                )
            )
            hidden = hidden + scale_row[:, None] * summed
        result = hidden.astype(jnp.bfloat16)
        grad_hidden = tangent.astype(jnp.float32)
        big_new = list(big_acc)
        small_new = list(small_acc)
        for layer_at in reversed(range(layers)):
            (
                hidden_in,
                root_row,
                normed,
                gathered,
                pullback,
                gated_val,
                scale_row,
                weighted,
                summed,
            ) = records[layer_at]
            gathered = fetch_layer(layer_at)
            zx_full, bc_full, dt_full, out_full = gathered
            params = tuple((item[layer_at] for item in smalls))
            grad_summed = (scale_row[:, None] * grad_hidden).astype(jnp.bfloat16)
            grad_scale = jnp.sum(grad_hidden * summed, axis=-1)
            out_term = jnp.einsum(
                "ti,td->id", weighted, grad_summed, preferred_element_type=jnp.float32
            )
            grad_weighted = jnp.einsum(
                "td,id->ti", grad_summed, out_full, preferred_element_type=jnp.float32
            )
            gain_term = jnp.sum(grad_weighted * gated_val, axis=0)
            grad_gated = (
                grad_weighted * params[8][None, :]
                - (grad_scale * scale_row**3 / inner_total)[:, None] * gated_val
            )
            mixer_grads = pullback(grad_gated)
            grad_both = jnp.stack([mixer_grads[0], mixer_grads[1]], axis=1).astype(jnp.bfloat16)
            grad_state = mixer_grads[2]
            grad_step = mixer_grads[3].astype(jnp.bfloat16)
            zx_term = jnp.einsum(
                "td,tki->kdi", normed, grad_both, preferred_element_type=jnp.float32
            )
            dt_term = jnp.einsum("td,th->dh", normed, grad_step, preferred_element_type=jnp.float32)
            bc_term = jnp.einsum(
                "td,tn->dn", normed.astype(jnp.float32), grad_state, precision=HIGH
            )
            normed_part = jnp.einsum(
                "tki,kdi->td", grad_both, zx_full, preferred_element_type=jnp.float32
            )
            normed_part = normed_part + jnp.einsum(
                "th,dh->td", grad_step, dt_full, preferred_element_type=jnp.float32
            )
            normed_part = normed_part + jnp.einsum(
                "tn,dn->td", grad_state, bc_full.astype(jnp.float32), precision=HIGH
            )
            grad_normed = lax.psum(normed_part.astype(jnp.bfloat16), "mp").astype(jnp.float32)
            unit_rows = hidden_in * root_row[:, None]
            norm_term = jnp.sum(grad_normed * unit_rows, axis=0)
            back_rows = grad_normed * params[0][None, :]
            grad_hidden = grad_hidden + root_row[:, None] * (
                back_rows - unit_rows * jnp.mean(back_rows * unit_rows, axis=-1, keepdims=True)
            )
            layer_terms = (zx_term, bc_term, dt_term, out_term)
            big_new[layer_at] = tuple(
                (big_acc[layer_at][which] + layer_terms[which] for which in range(4))
            )
            small_terms = (
                norm_term,
                mixer_grads[4],
                mixer_grads[5],
                mixer_grads[6],
                mixer_grads[7],
                mixer_grads[8],
                mixer_grads[9],
                mixer_grads[10],
                gain_term,
            )
            small_new[layer_at] = tuple(
                (small_acc[layer_at][which] + small_terms[which] for which in range(9))
            )
        return ((tuple(big_new), tuple(small_new)), (result, grad_hidden))

    (big_layers, small_layers), (outputs, input_grads) = lax.scan(
        micro_step, (big_init, small_init), (block_input, cotangent)
    )
    big_acc = tuple(
        (
            jnp.stack([big_layers[layer_at][which] for layer_at in range(layers)], axis=0)
            for which in range(4)
        )
    )
    small_acc = tuple(
        (
            jnp.stack([small_layers[layer_at][which] for layer_at in range(layers)], axis=0)
            for which in range(9)
        )
    )
    big_acc = (
        lax.psum_scatter(
            big_acc[0].astype(jnp.bfloat16), "dp", scatter_dimension=2, tiled=True
        ).astype(jnp.float32),
        lax.psum_scatter(
            big_acc[1].astype(jnp.bfloat16), "dp", scatter_dimension=1, tiled=True
        ).astype(jnp.float32),
        lax.psum_scatter(
            big_acc[2].astype(jnp.bfloat16), "dp", scatter_dimension=1, tiled=True
        ).astype(jnp.float32),
        lax.psum_scatter(
            big_acc[3].astype(jnp.bfloat16), "dp", scatter_dimension=2, tiled=True
        ).astype(jnp.float32),
    )
    small_sum = (
        lax.psum(small_acc[0].astype(jnp.bfloat16), "dp").astype(jnp.float32),
        lax.psum(small_acc[1].astype(jnp.bfloat16), "dp").astype(jnp.float32),
        lax.psum(small_acc[2].astype(jnp.bfloat16), "dp").astype(jnp.float32),
        lax.psum(small_acc[3].astype(jnp.bfloat16), "dp").astype(jnp.float32),
        lax.psum(small_acc[4].astype(jnp.bfloat16), "dp").astype(jnp.float32),
        lax.psum(small_acc[5].astype(jnp.bfloat16), "dp").astype(jnp.float32),
        lax.psum(small_acc[6].astype(jnp.bfloat16), "dp").astype(jnp.float32),
        lax.psum(small_acc[7].astype(jnp.bfloat16), "dp").astype(jnp.float32),
        lax.psum(small_acc[8].astype(jnp.bfloat16), "dp").astype(jnp.float32),
    )
    shared = (
        lax.psum(big_acc[1].astype(jnp.bfloat16), "mp").astype(jnp.float32),
        lax.psum(small_sum[3].astype(jnp.bfloat16), "mp").astype(jnp.float32),
        lax.psum(small_sum[4].astype(jnp.bfloat16), "mp").astype(jnp.float32),
    )
    norm_grad_out = small_sum[0]
    return (
        outputs,
        input_grads,
        big_acc[0],
        shared[0],
        big_acc[2],
        big_acc[3],
        norm_grad_out,
        small_sum[1],
        small_sum[2],
        shared[1],
        shared[2],
        small_sum[5],
        small_sum[6],
        small_sum[7],
        small_sum[8],
    )


def solution(mesh):
    placed = (
        P("dp", None, None),
        P(None, None, "dp", "mp"),
        P(None, "dp", None),
        P(None, "dp", "mp"),
        P(None, "mp", "dp"),
        P(),
        P(None, None, "mp"),
        P(None, "mp"),
        P(),
        P(),
        P(None, "mp"),
        P(None, "mp"),
        P(None, "mp"),
        P(None, "mp"),
        P("dp", None, None),
    )
    return jax.shard_map(
        per_device,
        mesh=mesh,
        in_specs=placed,
        out_specs=(
            P("dp", None, None),
            P("dp", None, None),
            P(None, None, "dp", "mp"),
            P(None, "dp", None),
            P(None, "dp", "mp"),
            P(None, "mp", "dp"),
            P(),
            P(None, None, "mp"),
            P(None, "mp"),
            P(),
            P(),
            P(None, "mp"),
            P(None, "mp"),
            P(None, "mp"),
            P(None, "mp"),
        ),
        check_vma=False,
    )
```

profile of v0, /device:TPU:0, one launch (start us, length us, event | category | flops | bytes accessed | tf_op | source)
XLA Modules:
  0.0 2879.8 jit_solution(3162141945582624290)
XLA Ops:
  11.8 2425.1 %while.274 = (s32[]{:T(128)}, f32[2,1536,768]{1,2,0:T(8,128)}, f32[1536,256]{1,0:T(8,128)}, f32[1536,12]{0,1:T(8,128)}, f32[768,1536]{1,0:T(8,128)}, /*index=5*/...) while((s32[]{:T(128)}, f32[2,1536,768]{1,2,0:T(8,128)}, ...), condition=%wide.region_81.83_spmd.clone, body=%wide.region_0.82_spmd.clone.sunk | while | flops 73711378432 | bytes 1355797888 | solution.py:291
  20.8 36.3 %all-gather.26 = bf16[1,1536,256]{2,1,0:T(8,128)(2,1)S(1)} all-gather(bf16[1,192,256]{2,1,0:T(8,128)(2,1)S(1)} %get-tuple-element.4301), channel_id=4, replica_groups=mesh['dp'=8,'mp'=4] {'dp'}, dimensions={1}, use_global_device_ids=true | all-gather | bytes 884736 | tf_op jit(solution)/shard_map/while/body/eval_jaxpr/all_gather | solution.py:98
  64.9 35.4 %all-gather.25 = bf16[1,1536,12]{2,0,1:T(2,128)(2,1)S(1)} all-gather(bf16[1,192,12]{2,0,1:T(2,128)(2,1)S(1)} %get-tuple-element.4298), channel_id=2, replica_groups=mesh['dp'=8,'mp'=4] {'dp'}, dimensions={1}, use_global_device_ids=true | all-gather | bytes 41472 | tf_op jit(solution)/shard_map/while/body/eval_jaxpr/all_gather | solution.py:99
  107.7 10.5 all-gather.37.cloned.1.call-done
  118.2 8.1 fusion.563
  137.9 56.1 %while.275 = (s32[]{:T(128)}, f32[12,64,128]{2,1,0:T(8,128)S(1)}, f32[4,256,768]{2,1,0:T(8,128)}, f32[4,12,64,128]{3,2,1,0:T(8,128)}, f32[4,256,12]{1,0,2:T(4,12...) while((s32[]{:T(128)}, f32[12,64,128]{2,1,0:T(8,128)S(1)}, ...), condition=%wide.region_5.6_spmd.clone, body=%wide.region_2.5_spmd.clone.sunk | while | flops 1314169856 | bytes 12615869 | solution.py:55
  198.8 6.7 convolution_convert_fusion.4
  206.8 34.1 %all-gather.30 = bf16[1,1536,256]{2,1,0:T(8,128)(2,1)} all-gather(bf16[1,192,256]{2,1,0:T(8,128)(2,1)S(1)} %copy-done.66), channel_id=8, replica_groups=mesh['dp'=8,'mp'=4] {'dp'}, dimensions={1}, use_global_device_ids=true | all-gather | bytes 884736 | tf_op jit(solution)/shard_map/while/body/eval_jaxpr/all_gather | solution.py:98
  240.9 32.0 %all-gather.28 = bf16[1,1536,12]{2,0,1:T(2,128)(2,1)S(1)} all-gather(bf16[1,192,12]{2,0,1:T(2,128)(2,1)S(1)} %copy-done.67), channel_id=6, replica_groups=mesh['dp'=8,'mp'=4] {'dp'}, dimensions={1}, use_global_device_ids=true | all-gather | bytes 41472 | tf_op jit(solution)/shard_map/while/body/eval_jaxpr/all_gather | solution.py:99
  289.3 64.7 %all-gather.41.cloned.1.call-done = bf16[1,2,1536,768]{3,2,1,0:T(8,128)(2,1)} async-done(((bf16[1,2,192,768]{3,2,1,0:T(8,128)(2,1)}), bf16[1,2,1536,768]{3,2,1,0:T(8,128)(2,1)}) %all-gather.41.cloned.1.call-update) | async-done | bytes 4718608 | tf_op jit(solution)/shard_map/while/body/eval_jaxpr/all_gather | solution.py:97
  354.0 7.1 fusion.573
  382.4 56.1 %while.276 = (s32[]{:T(128)}, f32[12,64,128]{2,1,0:T(8,128)S(1)}, f32[4,256,768]{2,1,0:T(8,128)}, f32[4,12,64,128]{3,2,1,0:T(8,128)}, f32[4,256,12]{1,0,2:T(4,12...) while((s32[]{:T(128)}, f32[12,64,128]{2,1,0:T(8,128)S(1)}, ...), condition=%wide.region_13.14_spmd.clone, body=%wide.region_10.13_spmd.clone.sunk | while | flops 1314169856 | bytes 12615869 | solution.py:55
  443.3 6.8 convolution_convert_fusion.5
  455.9 61.2 %all-reduce.54.cloned.1.call-done = bf16[1024,1536]{1,0:T(8,128)(2,1)} async-done(((bf16[1024,1536]{1,0:T(8,128)(2,1)}), bf16[1024,1536]{1,0:T(8,128)(2,1)}) %all-reduce.54.cloned.1.call-update) | async-done | bytes 3145744 | tf_op jit(solution)/shard_map/while/body/eval_jaxpr/psum | solution.py:197
  521.8 10.1 multiply_reduce_fusion.45
  536.3 218.9 %while.277 = (s32[]{:T(128)}, f32[12]{0:T(128)}, f32[12,64,128]{2,1,0:T(8,128)S(1)}, f32[4,256,768]{2,1,0:T(8,128)}, f32[4,256,12]{2,1,0:T(8,128)}, /*index=5*/f...) while((s32[]{:T(128)}, f32[12]{0:T(128)}, ...), condition=%wide.region_31.32_spmd.clone, body=%wide.region_18.31_spmd.clone.sunk | while | flops 3038917632 | bytes 28020556 | solution.py:55
  779.7 7.1 fusion.582
  799.5 7.1 select_add_fusion.27
  814.7 7.7 bitcast_add_fusion.15
  822.4 37.8 %all-reduce.56.cloned.1.call-done = bf16[1024,1536]{1,0:T(8,128)(2,1)} async-done(((bf16[1024,1536]{1,0:T(8,128)(2,1)}), bf16[1024,1536]{1,0:T(8,128)(2,1)}) %all-reduce.56.cloned.1.call-update) | async-done | bytes 3145744 | tf_op jit(solution)/shard_map/while/body/eval_jaxpr/psum | solution.py:264
  871.9 11.5 multiply_reduce_fusion.48
  887.8 218.3 %while.278 = (s32[]{:T(128)}, f32[12]{0:T(128)}, f32[12,64,128]{2,1,0:T(8,128)S(1)}, f32[4,256,768]{2,1,0:T(8,128)}, f32[4,256,12]{2,1,0:T(8,128)}, /*index=5*/f...) while((s32[]{:T(128)}, f32[12]{0:T(128)}, ...), condition=%wide.region_48.49_spmd.clone, body=%wide.region_35.48_spmd.clone.sunk | while | flops 3038917632 | bytes 28020556 | solution.py:55
  1106.1 9.2 multiply_reduce_fusion.49
  1131.9 7.0 fusion.590
  1144.7 8.7 select_add_fusion.26
  1155.1 7.1 convolution_add_fusion.22
  1162.3 10.0 bitcast_add_fusion.14
  1172.3 40.5 %all-reduce.58.cloned.1.call-done = bf16[1024,1536]{1,0:T(8,128)(2,1)} async-done(((bf16[1024,1536]{1,0:T(8,128)(2,1)}), bf16[1024,1536]{1,0:T(8,128)(2,1)}) %all-reduce.58.cloned.1.call-update) | async-done | bytes 3145744 | tf_op jit(solution)/shard_map/while/body/eval_jaxpr/psum | solution.py:264
  1232.4 34.7 %all-gather.26 = bf16[1,1536,256]{2,1,0:T(8,128)(2,1)S(1)} all-gather(bf16[1,192,256]{2,1,0:T(8,128)(2,1)S(1)} %get-tuple-element.4301), channel_id=4, replica_groups=mesh['dp'=8,'mp'=4] {'dp'}, dimensions={1}, use_global_device_ids=true | all-gather | bytes 884736 | tf_op jit(solution)/shard_map/while/body/eval_jaxpr/all_gather | solution.py:98
  1275.2 35.0 %all-gather.25 = bf16[1,1536,12]{2,0,1:T(2,128)(2,1)S(1)} all-gather(bf16[1,192,12]{2,0,1:T(2,128)(2,1)S(1)} %get-tuple-element.4298), channel_id=2, replica_groups=mesh['dp'=8,'mp'=4] {'dp'}, dimensions={1}, use_global_device_ids=true | all-gather | bytes 41472 | tf_op jit(solution)/shard_map/while/body/eval_jaxpr/all_gather | solution.py:99
  1317.6 9.5 all-gather.37.cloned.1.call-done
  1327.1 8.1 fusion.563
  1346.9 56.1 %while.275 = (s32[]{:T(128)}, f32[12,64,128]{2,1,0:T(8,128)S(1)}, f32[4,256,768]{2,1,0:T(8,128)}, f32[4,12,64,128]{3,2,1,0:T(8,128)}, f32[4,256,12]{1,0,2:T(4,12...) while((s32[]{:T(128)}, f32[12,64,128]{2,1,0:T(8,128)S(1)}, ...), condition=%wide.region_5.6_spmd.clone, body=%wide.region_2.5_spmd.clone.sunk | while | flops 1314169856 | bytes 12615869 | solution.py:55
  1407.7 6.7 convolution_convert_fusion.4
  1415.9 34.2 %all-gather.30 = bf16[1,1536,256]{2,1,0:T(8,128)(2,1)} all-gather(bf16[1,192,256]{2,1,0:T(8,128)(2,1)S(1)} %copy-done.66), channel_id=8, replica_groups=mesh['dp'=8,'mp'=4] {'dp'}, dimensions={1}, use_global_device_ids=true | all-gather | bytes 884736 | tf_op jit(solution)/shard_map/while/body/eval_jaxpr/all_gather | solution.py:98
  1450.1 32.3 %all-gather.28 = bf16[1,1536,12]{2,0,1:T(2,128)(2,1)S(1)} all-gather(bf16[1,192,12]{2,0,1:T(2,128)(2,1)S(1)} %copy-done.67), channel_id=6, replica_groups=mesh['dp'=8,'mp'=4] {'dp'}, dimensions={1}, use_global_device_ids=true | all-gather | bytes 41472 | tf_op jit(solution)/shard_map/while/body/eval_jaxpr/all_gather | solution.py:99
  1498.8 64.2 %all-gather.41.cloned.1.call-done = bf16[1,2,1536,768]{3,2,1,0:T(8,128)(2,1)} async-done(((bf16[1,2,192,768]{3,2,1,0:T(8,128)(2,1)}), bf16[1,2,1536,768]{3,2,1,0:T(8,128)(2,1)}) %all-gather.41.cloned.1.call-update) | async-done | bytes 4718608 | tf_op jit(solution)/shard_map/while/body/eval_jaxpr/all_gather | solution.py:97
  1563.0 7.1 fusion.573
  1591.4 56.1 %while.276 = (s32[]{:T(128)}, f32[12,64,128]{2,1,0:T(8,128)S(1)}, f32[4,256,768]{2,1,0:T(8,128)}, f32[4,12,64,128]{3,2,1,0:T(8,128)}, f32[4,256,12]{1,0,2:T(4,12...) while((s32[]{:T(128)}, f32[12,64,128]{2,1,0:T(8,128)S(1)}, ...), condition=%wide.region_13.14_spmd.clone, body=%wide.region_10.13_spmd.clone.sunk | while | flops 1314169856 | bytes 12615869 | solution.py:55
  1652.3 6.8 convolution_convert_fusion.5
  1664.8 61.2 %all-reduce.54.cloned.1.call-done = bf16[1024,1536]{1,0:T(8,128)(2,1)} async-done(((bf16[1024,1536]{1,0:T(8,128)(2,1)}), bf16[1024,1536]{1,0:T(8,128)(2,1)}) %all-reduce.54.cloned.1.call-update) | async-done | bytes 3145744 | tf_op jit(solution)/shard_map/while/body/eval_jaxpr/psum | solution.py:197
  1730.8 10.1 multiply_reduce_fusion.45
  1745.3 218.9 %while.277 = (s32[]{:T(128)}, f32[12]{0:T(128)}, f32[12,64,128]{2,1,0:T(8,128)S(1)}, f32[4,256,768]{2,1,0:T(8,128)}, f32[4,256,12]{2,1,0:T(8,128)}, /*index=5*/f...) while((s32[]{:T(128)}, f32[12]{0:T(128)}, ...), condition=%wide.region_31.32_spmd.clone, body=%wide.region_18.31_spmd.clone.sunk | while | flops 3038917632 | bytes 28020556 | solution.py:55
  1988.7 7.1 fusion.582
  2002.3 6.5 convolution_add_fusion.24
  2009.0 7.8 select_add_fusion.27
  2024.9 10.0 bitcast_add_fusion.15
  2034.9 34.3 %all-reduce.56.cloned.1.call-done = bf16[1024,1536]{1,0:T(8,128)(2,1)} async-done(((bf16[1024,1536]{1,0:T(8,128)(2,1)}), bf16[1024,1536]{1,0:T(8,128)(2,1)}) %all-reduce.56.cloned.1.call-update) | async-done | bytes 3145744 | tf_op jit(solution)/shard_map/while/body/eval_jaxpr/psum | solution.py:264
  2080.9 11.5 multiply_reduce_fusion.48
  2096.8 218.3 %while.278 = (s32[]{:T(128)}, f32[12]{0:T(128)}, f32[12,64,128]{2,1,0:T(8,128)S(1)}, f32[4,256,768]{2,1,0:T(8,128)}, f32[4,256,12]{2,1,0:T(8,128)}, /*index=5*/f...) while((s32[]{:T(128)}, f32[12]{0:T(128)}, ...), condition=%wide.region_48.49_spmd.clone, body=%wide.region_35.48_spmd.clone.sunk | while | flops 3038917632 | bytes 28020556 | solution.py:55
  2315.1 9.2 multiply_reduce_fusion.49
  2340.9 7.0 fusion.590
  2353.7 10.3 select_add_fusion.26
  2365.7 7.6 convolution_add_fusion.22
  2373.4 11.5 bitcast_add_fusion.14
  2384.8 36.9 %all-reduce.58.cloned.1.call-done = bf16[1024,1536]{1,0:T(8,128)(2,1)} async-done(((bf16[1024,1536]{1,0:T(8,128)(2,1)}), bf16[1024,1536]{1,0:T(8,128)(2,1)}) %all-reduce.58.cloned.1.call-update) | async-done | bytes 3145744 | tf_op jit(solution)/shard_map/while/body/eval_jaxpr/psum | solution.py:264
  2450.6 56.1 %reduce-scatter.9.cloned.1.call-done = bf16[2,192,256]{2,1,0:T(8,128)(2,1)} async-done(((bf16[2,1536,256]{2,1,0:T(8,128)(2,1)}), bf16[2,192,256]{2,1,0:T(8,128)(2,1)}) %reduce-scatter.9.cloned.1.call-update) | async-done | bytes 196624 | tf_op jit(solution)/shard_map/reduce_scatter | solution.py:310
  2511.2 7.7 copy.350
  2518.8 7.7 copy.349
  2526.5 8.3 pad_maximum_fusion.6
  2536.2 34.8 %all-reduce.42 = (bf16[2,1536]{1,0:T(2,128)(2,1)S(1)}, bf16[2,4,768]{2,1,0:T(4,128)(2,1)S(1)}, bf16[2,768]{1,0:T(2,128)(2,1)S(1)}, bf16[2,4,256]{2,1,0:T(4,128)(...) all-reduce(bf16[2,1536]{1,0:T(2,128)(2,1)S(1)} %pad_maximum_fusion., ...), channel_id=1, replica_groups=mesh['dp'=8,'mp'=4] {'dp'}, use_global_device_ids=true, to_apply=%region_87.89 | all-reduce | flops 14920 | bytes 59680 | tf_op jit(solution)/shard_map/psum | solution.py:321
  2583.6 21.0 all-reduce.50.cloned.1.call-done
  2606.4 97.7 %reduce-scatter.11.cloned.1.call-done = bf16[2,768,192]{1,2,0:T(8,128)(2,1)} async-done(((bf16[2,768,1536]{1,2,0:T(8,128)(2,1)}), bf16[2,768,192]{1,2,0:T(8,128)(2,1)}) %reduce-scatter.11.cloned.1.call-update) | async-done | bytes 589840 | tf_op jit(solution)/shard_map/reduce_scatter | solution.py:316
  2706.2 163.1 %reduce-scatter.7.cloned.1.call-done = bf16[2,2,192,768]{3,2,1,0:T(8,128)(2,1)} async-done(((bf16[2,2,1536,768]{3,2,1,0:T(8,128)(2,1)}), bf16[2,2,192,768]{3,2,1,0:T(8,128)(2,1)}) %reduce-scatter.7.cloned.1.call-update) | async-done | bytes 1179664 | tf_op jit(solution)/shard_map/reduce_scatter | solution.py:307
  (2819 shorter events, 1514.1 us)
Async XLA Ops:
  12.0 52.1 %copy-start.55 = (bf16[2,192,12]{2,0,1:T(2,128)(2,1)}, bf16[2,192,12]{2,0,1:T(2,128)(2,1)S(1)}, u32[]{:S(2)}) copy-start(bf16[2,192,12]{2,0,1:T(2,128)(2,1)S(1)} %get-tuple-element.4878) | copy-start | bytes 27652 | tf_op jit(solution)/shard_map/while
  12.0 106.2 %all-gather.37.cloned.1.call-start = ((), (), s32[]{:S(2)}) async-start(), calls=%async_computation.9 | async-start | bytes 5308416 | tf_op jit(solution)/shard_map/while/body/eval_jaxpr/all_gather | solution.py:97
  14.6 42.5 %copy-start.163 = (f32[2,4,256]{2,1,0:T(4,128)S(1)}, f32[2,4,256]{2,1,0:T(4,128)}, u32[]{:S(2)}) copy-start(f32[2,4,256]{2,1,0:T(4,128)} %get-tuple-element.4881) | copy-start | bytes 24580 | tf_op jit(solution)/shard_map/while
  14.6 43.2 %copy-start.196 = (f32[2,256]{1,0:T(2,128)S(1)}, f32[2,256]{1,0:T(2,128)}, u32[]{:S(2)}) copy-start(f32[2,256]{1,0:T(2,128)} %get-tuple-element.4880) | copy-start | bytes 6148 | tf_op jit(solution)/shard_map/while
  14.6 184.2 %all-gather.39.cloned.1.call-start = ((), (), s32[]{:S(2)}) async-start(), calls=%async_computation.10 | async-start | bytes 2654208 | tf_op jit(solution)/shard_map/while/body/eval_jaxpr/all_gather | solution.py:100
  15.5 265.3 %all-reduce.52.cloned.1.call-start = ((), (), s32[]{:S(2)}) async-start(), calls=%async_computation.11 | async-start | bytes 6291456 | tf_op jit(solution)/shard_map/while/body/eval_jaxpr/psum | solution.py:197
  18.8 99.4 %copy-start.116 = (f32[1024]{0:T(1024)}, f32[1024]{0:T(1024)S(1)}, u32[]{:S(2)}) copy-start(f32[1024]{0:T(1024)S(1)} %add_rsqrt_fusion.8) | copy-start | bytes 12292 | tf_op jit(solution)/shard_map/while
  18.9 99.3 %copy-start.81 = (f32[1536]{0:T(1024)}, f32[1536]{0:T(1024)S(1)}, u32[]{:S(2)}) copy-start(f32[1536]{0:T(1024)S(1)} %get-tuple-element.4290) | copy-start | bytes 18436 | tf_op jit(solution)/shard_map/while
  18.9 266.8 %copy-start.79 = (f32[1536]{0:T(1024)}, f32[1536]{0:T(1024)S(1)}, u32[]{:S(2)}) copy-start(f32[1536]{0:T(1024)S(1)} %get-tuple-element.4318) | copy-start | bytes 18436 | tf_op jit(solution)/shard_map/while
  19.6 109.4 %copy-start.96 = (f32[768]{0:T(1024)}, f32[768]{0:T(1024)S(1)}, u32[]{:S(2)}) copy-start(f32[768]{0:T(1024)S(1)} %get-tuple-element.4291) | copy-start | bytes 9220 | tf_op jit(solution)/shard_map/while
  61.5 39.7 %copy-start.204 = (f32[2,12]{1,0:T(2,128)S(1)}, f32[2,12]{1,0:T(2,128)}, u32[]{:S(2)}) copy-start(f32[2,12]{1,0:T(2,128)} %get-tuple-element.4879) | copy-start | bytes 292 | tf_op jit(solution)/shard_map/while
  101.2 25.2 copy-start.73
  107.7 413.2 %copy-start.71 = (f32[768]{0:T(1024)}, f32[768]{0:T(1024)S(1)}, u32[]{:S(2)}) copy-start(f32[768]{0:T(1024)S(1)} %get-tuple-element.4344) | copy-start | bytes 9220 | tf_op jit(solution)/shard_map/while
  137.9 56.1 %copy-start.112 = (f32[768]{0:T(1024)S(1)}, f32[768]{0:T(1024)}, u32[]{:S(2)}) copy-start(f32[768]{0:T(1024)} %mul.4047) | copy-start | bytes 9220 | tf_op jit(solution)/shard_map/while
  205.5 35.4 %copy-start.67 = (bf16[1,192,12]{2,0,1:T(2,128)(2,1)S(1)}, bf16[1,192,12]{2,0,1:T(2,128)(2,1)}, u32[]{:S(2)}) copy-start(bf16[1,192,12]{2,0,1:T(2,128)(2,1)} %get-tuple-element.4316) | copy-start | bytes 13828 | tf_op jit(solution)/shard_map/while
  205.5 68.9 %copy-start.197 = (f32[12]{0:T(128)S(1)}, f32[12]{0:T(128)}, u32[]{:S(2)}) copy-start(f32[12]{0:T(128)} %get-tuple-element.4340) | copy-start | bytes 148 | tf_op jit(solution)/shard_map/while
  205.5 148.5 %all-gather.41.cloned.1.call-start = ((), (), s32[]{:S(2)}) async-start(), calls=%async_computation.12 | async-start | bytes 5308416 | tf_op jit(solution)/shard_map/while/body/eval_jaxpr/all_gather | solution.py:97
  206.1 237.2 %all-gather.43.cloned.1.call-start = ((), (), s32[]{:S(2)}) async-start(), calls=%async_computation.13 | async-start | bytes 2654208 | tf_op jit(solution)/shard_map/while/body/eval_jaxpr/all_gather | solution.py:100
  206.7 310.4 %all-reduce.54.cloned.1.call-start = ((), (), s32[]{:S(2)}) async-start(), calls=%async_computation.14 | async-start | bytes 6291456 | tf_op jit(solution)/shard_map/while/body/eval_jaxpr/psum | solution.py:197
  289.3 86.8 %copy-start.2 = (bf16[1024,1536]{1,0:T(8,128)(2,1)}, bf16[1024,1536]{1,0:T(8,128)(2,1)S(1)}, u32[]{:S(2)}) copy-start(bf16[1024,1536]{1,0:T(8,128)(2,1)S(1)} %multiply_convert_fusion.25) | copy-start | bytes 9437188 | tf_op jit(solution)/shard_map/while
  382.4 56.1 %copy-start.114 = (f32[768]{0:T(1024)S(1)}, f32[768]{0:T(1024)}, u32[]{:S(2)}) copy-start(f32[768]{0:T(1024)} %mul.4048) | copy-start | bytes 9220 | tf_op jit(solution)/shard_map/while
  443.2 77.7 %copy-start.18 = (f32[1024,768]{1,0:T(8,128)}, f32[1024,768]{1,0:T(8,128)S(1)}, u32[]{:S(2)}) copy-start(f32[1024,768]{1,0:T(8,128)S(1)} %get-tuple-element.4341) | copy-start | bytes 9437188 | tf_op jit(solution)/shard_map/while
  450.1 410.1 %all-reduce.56.cloned.1.call-start = ((), (), s32[]{:S(2)}) async-start(), calls=%async_computation.15 | async-start | bytes 6291456 | tf_op jit(solution)/shard_map/while/body/eval_jaxpr/psum | solution.py:264
  569.4 12.3 copy-start.60
  678.6 12.3 copy-start.60
  791.5 421.3 %all-reduce.58.cloned.1.call-start = ((), (), s32[]{:S(2)}) async-start(), calls=%async_computation.16 | async-start | bytes 6291456 | tf_op jit(solution)/shard_map/while/body/eval_jaxpr/psum | solution.py:264
  814.7 45.5 %copy-start.80 = (f32[1536]{0:T(1024)S(1)}, f32[1536]{0:T(1024)}, u32[]{:S(2)}) copy-start(f32[1536]{0:T(1024)} %copy-done.79) | copy-start | bytes 18436 | tf_op jit(solution)/shard_map/while
  814.7 45.5 %copy-start.84 = (f32[1024]{0:T(1024)S(1)}, f32[1024]{0:T(1024)}, u32[]{:S(2)}) copy-start(f32[1024]{0:T(1024)} %copy-done.83) | copy-start | bytes 12292 | tf_op jit(solution)/shard_map/while
  1139.0 14.5 slice-start
  1172.3 44.8 %copy-start.141 = (f32[1536]{0:T(1024)S(1)}, f32[1536]{0:T(1024)}, u32[]{:S(2)}) copy-start(f32[1536]{0:T(1024)} %get-tuple-element.4787) | copy-start | bytes 18436 | tf_op jit(solution)/shard_map/while
  1223.6 50.8 %copy-start.55 = (bf16[2,192,12]{2,0,1:T(2,128)(2,1)}, bf16[2,192,12]{2,0,1:T(2,128)(2,1)S(1)}, u32[]{:S(2)}) copy-start(bf16[2,192,12]{2,0,1:T(2,128)(2,1)S(1)} %get-tuple-element.4878) | copy-start | bytes 27652 | tf_op jit(solution)/shard_map/while
  1223.7 103.5 %all-gather.37.cloned.1.call-start = ((), (), s32[]{:S(2)}) async-start(), calls=%async_computation.9 | async-start | bytes 5308416 | tf_op jit(solution)/shard_map/while/body/eval_jaxpr/all_gather | solution.py:97
  1226.2 40.9 %copy-start.163 = (f32[2,4,256]{2,1,0:T(4,128)S(1)}, f32[2,4,256]{2,1,0:T(4,128)}, u32[]{:S(2)}) copy-start(f32[2,4,256]{2,1,0:T(4,128)} %get-tuple-element.4881) | copy-start | bytes 24580 | tf_op jit(solution)/shard_map/while
  1226.2 41.6 %copy-start.196 = (f32[2,256]{1,0:T(2,128)S(1)}, f32[2,256]{1,0:T(2,128)}, u32[]{:S(2)}) copy-start(f32[2,256]{1,0:T(2,128)} %get-tuple-element.4880) | copy-start | bytes 6148 | tf_op jit(solution)/shard_map/while
  1226.2 181.5 %all-gather.39.cloned.1.call-start = ((), (), s32[]{:S(2)}) async-start(), calls=%async_computation.10 | async-start | bytes 2654208 | tf_op jit(solution)/shard_map/while/body/eval_jaxpr/all_gather | solution.py:100
  1227.1 263.1 %all-reduce.52.cloned.1.call-start = ((), (), s32[]{:S(2)}) async-start(), calls=%async_computation.11 | async-start | bytes 6291456 | tf_op jit(solution)/shard_map/while/body/eval_jaxpr/psum | solution.py:197
  1230.4 96.7 %copy-start.116 = (f32[1024]{0:T(1024)}, f32[1024]{0:T(1024)S(1)}, u32[]{:S(2)}) copy-start(f32[1024]{0:T(1024)S(1)} %add_rsqrt_fusion.8) | copy-start | bytes 12292 | tf_op jit(solution)/shard_map/while
  1230.5 96.7 %copy-start.81 = (f32[1536]{0:T(1024)}, f32[1536]{0:T(1024)S(1)}, u32[]{:S(2)}) copy-start(f32[1536]{0:T(1024)S(1)} %get-tuple-element.4290) | copy-start | bytes 18436 | tf_op jit(solution)/shard_map/while
  1230.5 264.6 %copy-start.79 = (f32[1536]{0:T(1024)}, f32[1536]{0:T(1024)S(1)}, u32[]{:S(2)}) copy-start(f32[1536]{0:T(1024)S(1)} %get-tuple-element.4318) | copy-start | bytes 18436 | tf_op jit(solution)/shard_map/while
  1231.2 106.8 %copy-start.96 = (f32[768]{0:T(1024)}, f32[768]{0:T(1024)S(1)}, u32[]{:S(2)}) copy-start(f32[768]{0:T(1024)S(1)} %get-tuple-element.4291) | copy-start | bytes 9220 | tf_op jit(solution)/shard_map/while
  1271.8 39.1 %copy-start.204 = (f32[2,12]{1,0:T(2,128)S(1)}, f32[2,12]{1,0:T(2,128)}, u32[]{:S(2)}) copy-start(f32[2,12]{1,0:T(2,128)} %get-tuple-element.4879) | copy-start | bytes 292 | tf_op jit(solution)/shard_map/while
  1310.9 24.4 copy-start.73
  1317.6 412.4 %copy-start.71 = (f32[768]{0:T(1024)}, f32[768]{0:T(1024)S(1)}, u32[]{:S(2)}) copy-start(f32[768]{0:T(1024)S(1)} %get-tuple-element.4344) | copy-start | bytes 9220 | tf_op jit(solution)/shard_map/while
  1346.9 56.1 %copy-start.112 = (f32[768]{0:T(1024)S(1)}, f32[768]{0:T(1024)}, u32[]{:S(2)}) copy-start(f32[768]{0:T(1024)} %mul.4047) | copy-start | bytes 9220 | tf_op jit(solution)/shard_map/while
  1414.5 35.6 %copy-start.67 = (bf16[1,192,12]{2,0,1:T(2,128)(2,1)S(1)}, bf16[1,192,12]{2,0,1:T(2,128)(2,1)}, u32[]{:S(2)}) copy-start(bf16[1,192,12]{2,0,1:T(2,128)(2,1)} %get-tuple-element.4316) | copy-start | bytes 13828 | tf_op jit(solution)/shard_map/while
  1414.5 69.4 %copy-start.197 = (f32[12]{0:T(128)S(1)}, f32[12]{0:T(128)}, u32[]{:S(2)}) copy-start(f32[12]{0:T(128)} %get-tuple-element.4340) | copy-start | bytes 148 | tf_op jit(solution)/shard_map/while
  1414.5 148.5 %all-gather.41.cloned.1.call-start = ((), (), s32[]{:S(2)}) async-start(), calls=%async_computation.12 | async-start | bytes 5308416 | tf_op jit(solution)/shard_map/while/body/eval_jaxpr/all_gather | solution.py:97
  1415.1 237.2 %all-gather.43.cloned.1.call-start = ((), (), s32[]{:S(2)}) async-start(), calls=%async_computation.13 | async-start | bytes 2654208 | tf_op jit(solution)/shard_map/while/body/eval_jaxpr/all_gather | solution.py:100
  1415.8 310.2 %all-reduce.54.cloned.1.call-start = ((), (), s32[]{:S(2)}) async-start(), calls=%async_computation.14 | async-start | bytes 6291456 | tf_op jit(solution)/shard_map/while/body/eval_jaxpr/psum | solution.py:197
  1498.8 86.3 %copy-start.2 = (bf16[1024,1536]{1,0:T(8,128)(2,1)}, bf16[1024,1536]{1,0:T(8,128)(2,1)S(1)}, u32[]{:S(2)}) copy-start(bf16[1024,1536]{1,0:T(8,128)(2,1)S(1)} %multiply_convert_fusion.25) | copy-start | bytes 9437188 | tf_op jit(solution)/shard_map/while
  1591.4 56.1 %copy-start.114 = (f32[768]{0:T(1024)S(1)}, f32[768]{0:T(1024)}, u32[]{:S(2)}) copy-start(f32[768]{0:T(1024)} %mul.4048) | copy-start | bytes 9220 | tf_op jit(solution)/shard_map/while
  1652.2 77.8 %copy-start.18 = (f32[1024,768]{1,0:T(8,128)}, f32[1024,768]{1,0:T(8,128)S(1)}, u32[]{:S(2)}) copy-start(f32[1024,768]{1,0:T(8,128)S(1)} %get-tuple-element.4341) | copy-start | bytes 9437188 | tf_op jit(solution)/shard_map/while
  1659.1 410.1 %all-reduce.56.cloned.1.call-start = ((), (), s32[]{:S(2)}) async-start(), calls=%async_computation.15 | async-start | bytes 6291456 | tf_op jit(solution)/shard_map/while/body/eval_jaxpr/psum | solution.py:264
  1887.6 12.3 copy-start.60
  2000.5 421.3 %all-reduce.58.cloned.1.call-start = ((), (), s32[]{:S(2)}) async-start(), calls=%async_computation.16 | async-start | bytes 6291456 | tf_op jit(solution)/shard_map/while/body/eval_jaxpr/psum | solution.py:264
  2024.9 44.3 %copy-start.80 = (f32[1536]{0:T(1024)S(1)}, f32[1536]{0:T(1024)}, u32[]{:S(2)}) copy-start(f32[1536]{0:T(1024)} %copy-done.79) | copy-start | bytes 18436 | tf_op jit(solution)/shard_map/while
  2024.9 44.3 %copy-start.84 = (f32[1024]{0:T(1024)S(1)}, f32[1024]{0:T(1024)}, u32[]{:S(2)}) copy-start(f32[1024]{0:T(1024)} %copy-done.83) | copy-start | bytes 12292 | tf_op jit(solution)/shard_map/while
  2348.0 16.0 slice-start
  2384.8 41.2 %copy-start.141 = (f32[1536]{0:T(1024)S(1)}, f32[1536]{0:T(1024)}, u32[]{:S(2)}) copy-start(f32[1536]{0:T(1024)} %get-tuple-element.4787) | copy-start | bytes 18436 | tf_op jit(solution)/shard_map/while
  2436.9 69.8 %reduce-scatter.9.cloned.1.call-start = ((), (), s32[]{:S(2)}) async-start(), calls=%async_computation.5 | async-start | bytes 1769472 | tf_op jit(solution)/shard_map/reduce_scatter | solution.py:310
  2440.3 141.7 %reduce-scatter.13.cloned.1.call-start = ((), (), s32[]{:S(2)}) async-start(), calls=%async_computation.8 | async-start | bytes 442368
  2442.2 162.4 %all-reduce.50.cloned.1.call-start = ((), (), s32[]{:S(2)}) async-start(), calls=%async_computation.6 | async-start | bytes 393216 | tf_op jit(solution)/shard_map/psum | solution.py:332
  2506.8 197.3 %reduce-scatter.11.cloned.1.call-start = ((), (), s32[]{:S(2)}) async-start(), calls=%async_computation.7 | async-start | bytes 5308416 | tf_op jit(solution)/shard_map/reduce_scatter | solution.py:316
  2511.1 358.3 %reduce-scatter.7.cloned.1.call-start = ((), (), s32[]{:S(2)}) async-start(), calls=%async_computation.4 | async-start | bytes 10616832 | tf_op jit(solution)/shard_map/reduce_scatter | solution.py:307
  (537 other events, 2553.2 us)
Sparse Core Ops, SparseCore 0:
  15.0 103.1 all-gather.36
  120.4 50.1 all-gather.38
  205.7 66.7 all-reduce.51
  274.5 79.4 all-gather.40
  356.6 50.1 all-gather.42
  450.2 66.8 all-reduce.53
  791.6 68.5 all-reduce.55
  1144.2 68.5 all-reduce.57
  1226.7 100.4 all-gather.36
  1329.2 50.1 all-gather.38
  1414.6 66.7 all-reduce.51
  1483.5 79.4 all-gather.40
  1565.7 50.0 all-gather.42
  1659.2 66.8 all-reduce.53
  2000.6 68.5 all-reduce.55
  2353.2 68.5 all-reduce.57
Sparse Core Ops, SparseCore 1:
  2440.8 65.9 reduce-scatter.8
  2510.5 61.2 reduce-scatter.12
  2573.9 30.8 all-reduce.49
  2608.3 95.7 reduce-scatter.10
  2707.7 161.6 reduce-scatter.6
where the time goes:
time: 2900 us; the launch traced here: 2880 us
  waiting for transfers between devices  762 us (26%)
  matrix products  749 us (26%)
  local copies, waits for them, and re-layouts  556 us (19%)
  other arithmetic  442 us (15%)
  blocking collectives  337 us (12%)
    dot_general x48, matrix products, one_block(): within = jnp.einsum('tsh,shp->thp', mixing, values, precision=HIGH)  244 us
    reduce_scatter x1, waiting for transfers between devices, per_device(): lax.psum_scatter(big_acc[0].astype(jnp.bfloat16), 'dp', scatter_dimension...  163 us
    psum x4, waiting for transfers between devices, micro_step(): lax.psum(normed_part.astype(jnp.bfloat16), 'mp').astype(jnp.float32)  149 us
    all_gather x4, waiting for transfers between devices, gather_layer(): lax.all_gather(zx_weight[layer_at], 'dp', axis=1, tiled=True)  149 us
    all_gather x4, blocking collectives, gather_layer(): lax.all_gather(bc_weight[layer_at], 'dp', axis=0, tiled=True)  139 us
    all_gather x4, blocking collectives, gather_layer(): lax.all_gather(dt_weight[layer_at], 'dp', axis=0, tiled=True)  135 us
    psum x4, waiting for transfers between devices, micro_step(): summed = lax.psum(partial_out, 'mp').astype(jnp.float32)  122 us
    another operation x248, local copies, waits for them, and re-layouts  111 us
  transfers between devices with their start and end apart: 21, of which 14 were waited for; matrix products, arithmetic and copies ran while one was open for 19% of the time, Pallas kernels for 0%

commit v1 on v0

v1 whole, which is shorter than its diff:
```python
import functools

import jax
import jax.numpy as jnp
from jax import lax
from jax.experimental import pallas as pl
from jax.experimental.pallas import tpu as pltpu
from jax.sharding import PartitionSpec as P

EPS = 1e-05
HIGH = lax.Precision.HIGHEST
CHUNK = 128
TAPS = 4
F32 = jnp.float32
BF16 = jnp.bfloat16


def dot_nn(a, b):
    return lax.dot_general(a, b, (((1,), (0,)), ((), ())), preferred_element_type=F32)


def dot_nt(a, b):
    return lax.dot_general(a, b, (((1,), (1,)), ((), ())), preferred_element_type=F32)


def dot_tn(a, b):
    return lax.dot_general(a, b, (((0,), (0,)), ((), ())), preferred_element_type=F32)


def sigmoid(v):
    return 0.5 * jnp.tanh(0.5 * v) + 0.5


def softplus(v):
    return jnp.maximum(v, 0.0) + jnp.log1p(jnp.exp(-jnp.abs(v)))


def lanes_of(shape):
    return lax.broadcasted_iota(jnp.int32, shape, 1)


def rows_of(shape):
    return lax.broadcasted_iota(jnp.int32, shape, 0)


def shifted_right(now, before, by):
    merged = jnp.where(lanes_of(now.shape) >= CHUNK - by, before, now)
    return pltpu.roll(merged, by, 1)


def shifted_left(now, after, by):
    merged = jnp.where(lanes_of(now.shape) < by, after, now)
    return pltpu.roll(merged, CHUNK - by, 1)


def decay_pieces(raw, bias, rate):
    step = softplus(raw + bias)
    upper = (rows_of((CHUNK, CHUNK)) <= lanes_of((CHUNK, CHUNK))).astype(F32)
    cum = lax.dot_general(
        step * rate, upper, (((1,), (0,)), ((), ())), precision=HIGH, preferred_element_type=F32
    )
    return step, cum


def transposed(a):
    rows = a.shape[0]
    padded = jnp.concatenate([a, jnp.zeros((CHUNK - rows, CHUNK), F32)], axis=0)
    return jnp.transpose(padded)


def forward_body(dims, z_ref, conv_ref, head_ref, row_ref, w_ref, sq_ref, y_ref, s_ref, act, tail, state, wide):
    inner, heads, width, states = dims
    chans = inner + 2 * states
    at = pl.program_id(0)

    @pl.when(at == 0)
    def _():
        tail[...] = jnp.zeros_like(tail)
        state[...] = jnp.zeros_like(state)
        for which in range(TAPS + 1):
            wide[which] = jnp.broadcast_to(conv_ref[:, which : which + 1], (chans, CHUNK))

    for row in range(0, chans, width):
        span = slice(row, row + width)
        now = z_ref[inner + row : inner + row + width, :].astype(F32)
        before = tail[span, :].astype(F32)
        conv = wide[TAPS, span, :] + wide[TAPS - 1, span, :] * now
        for by in range(1, TAPS):
            conv = conv + wide[TAPS - 1 - by, span, :] * shifted_right(now, before, by)
        act[span, :] = conv * sigmoid(conv)
    tail[...] = z_ref[inner : inner + chans, :]

    step, cum = decay_pieces(
        z_ref[inner + chans :, :].astype(F32), head_ref[:, 0:1], head_ref[:, 1:2]
    )
    cum_t = transposed(cum)
    key = act[inner : inner + states, :].astype(BF16)
    query = act[inner + states :, :].astype(BF16)
    scores = dot_tn(key, query)
    seen = rows_of((CHUNK, CHUNK)) <= lanes_of((CHUNK, CHUNK))
    grown = jnp.exp(cum)
    last = cum[:, CHUNK - 1 :]
    to_end = jnp.exp(last - cum) * step
    fade = jnp.broadcast_to(jnp.exp(last), cum.shape)
    squares = jnp.zeros((8, CHUNK), F32)
    s_ref[0] = state[...]
    for head in range(heads):
        span = slice(head * width, (head + 1) * width)
        gap = cum[head : head + 1, :] - cum_t[:, head : head + 1]
        mixing = (scores * jnp.exp(jnp.where(seen, gap, -1e30))).astype(BF16)
        x = act[span, :]
        held = state[span, :]
        scan = dot_nn((x * step[head : head + 1, :]).astype(BF16), mixing)
        scan = scan + grown[head : head + 1, :] * dot_nn(held.astype(BF16), query)
        y_ref[span, :] = scan
        state[span, :] = fade[head : head + 1, :] * held + dot_nt(
            (x * to_end[head : head + 1, :]).astype(BF16), key
        )
        gate = z_ref[span, :].astype(F32)
        gated = (scan + row_ref[span, 1:2] * x) * (gate * sigmoid(gate))
        squares = squares + jnp.sum((gated * gated).reshape(width // 8, 8, CHUNK), axis=0)
        w_ref[span, :] = (gated * row_ref[span, 0:1]).astype(BF16)
    sq_ref[...] = squares


def forward_mix(z, conv_cols, head_cols, row_cols, dims):
    inner, heads, width, states = dims
    chans = inner + 2 * states
    rows, length = z.shape
    count = length // CHUNK
    return pl.pallas_call(
        functools.partial(forward_body, dims),
        grid=(count,),
        in_specs=[
            pl.BlockSpec((rows, CHUNK), lambda c: (0, c)),
            pl.BlockSpec(conv_cols.shape, lambda c: (0, 0)),
            pl.BlockSpec(head_cols.shape, lambda c: (0, 0)),
            pl.BlockSpec(row_cols.shape, lambda c: (0, 0)),
        ],
        out_specs=[
            pl.BlockSpec((inner, CHUNK), lambda c: (0, c)),
            pl.BlockSpec((8, CHUNK), lambda c: (0, c)),
            pl.BlockSpec((inner, CHUNK), lambda c: (0, c)),
            pl.BlockSpec((1, inner, states), lambda c: (c, 0, 0)),
        ],
        out_shape=[
            jax.ShapeDtypeStruct((inner, length), BF16),
            jax.ShapeDtypeStruct((8, length), F32),
            jax.ShapeDtypeStruct((inner, length), F32),
            jax.ShapeDtypeStruct((count, inner, states), F32),
        ],
        scratch_shapes=[
            pltpu.VMEM((chans, CHUNK), F32),
            pltpu.VMEM((chans, CHUNK), BF16),
            pltpu.VMEM((inner, states), F32),
            pltpu.VMEM((TAPS + 1, chans, CHUNK), F32),
        ],
        cost_estimate=pl.CostEstimate(
            flops=2 * length * inner * (CHUNK + 2 * states) * 2,
            bytes_accessed=rows * length * 2 + inner * length * 6 + count * inner * states * 4,
            transcendentals=length * heads * CHUNK,
        ),
        name="mix_forward",
    )(z, conv_cols, head_cols, row_cols)


def backward_body(
    dims, z_ref, zp_ref, dw_ref, r_ref, y_ref, s_ref, conv_ref, head_ref, row_ref,
    dz_ref, chan_ref, inner_ref, hsum_ref,
    act, slope, shifts, later, snext, dstate, dact, wide, acc_c, acc_i, acc_h, prod,
):
    inner, heads, width, states = dims
    chans = inner + 2 * states
    hrows = head_ref.shape[0]
    at = pl.program_id(0)
    total = pl.num_programs(0)

    @pl.when(at == 0)
    def _():
        later[...] = jnp.zeros_like(later)
        snext[...] = jnp.zeros_like(snext)
        dstate[...] = jnp.zeros_like(dstate)
        acc_c[...] = jnp.zeros_like(acc_c)
        acc_i[...] = jnp.zeros_like(acc_i)
        acc_h[...] = jnp.zeros_like(acc_h)
        for which in range(TAPS + 1):
            wide[which] = jnp.broadcast_to(conv_ref[:, which : which + 1], (chans, CHUNK))

    started = jnp.where(at == total - 1, 0.0, 1.0)
    for row in range(0, chans, width):
        span = slice(row, row + width)
        now = z_ref[inner + row : inner + row + width, :].astype(F32)
        before = zp_ref[inner + row : inner + row + width, :].astype(F32) * started
        conv = wide[TAPS, span, :] + wide[TAPS - 1, span, :] * now
        for by in range(1, TAPS):
            moved = shifted_right(now, before, by)
            shifts[by - 1, span, :] = moved
            conv = conv + wide[TAPS - 1 - by, span, :] * moved
        sig = sigmoid(conv)
        out = conv * sig
        act[span, :] = out
        slope[span, :] = sig + out * (1.0 - sig)

    raw = z_ref[inner + chans :, :].astype(F32) + head_ref[:, 0:1]
    rate = head_ref[:, 1:2]
    step, cum = decay_pieces(raw, 0.0, rate)
    cum_t = transposed(cum)
    key = act[inner : inner + states, :].astype(BF16)
    query = act[inner + states :, :].astype(BF16)
    scores = dot_tn(key, query)
    seen = rows_of((CHUNK, CHUNK)) <= lanes_of((CHUNK, CHUNK))
    grown = jnp.exp(cum)
    last = cum[:, CHUNK - 1 :]
    to_end = jnp.exp(last - cum)
    fade = jnp.broadcast_to(jnp.exp(last), cum.shape)
    dscores = jnp.zeros((CHUNK, CHUNK), F32)
    dkey = jnp.zeros((states, CHUNK), F32)
    dquery = jnp.zeros((states, CHUNK), F32)
    weight_row = r_ref[0:1, :]
    for head in range(heads):
        span = slice(head * width, (head + 1) * width)
        one = slice(head, head + 1)
        x = act[span, :]
        gate = z_ref[span, :].astype(F32)
        sg = sigmoid(gate)
        sgate = gate * sg
        scan = y_ref[span, :]
        y = scan + row_ref[span, 1:2] * x
        gated = y * sgate
        dw = dw_ref[span, :].astype(F32)
        dgated = dw * row_ref[span, 0:1] - weight_row * gated
        acc_i[0, span, :] += dw * gated
        dy = dgated * sgate
        acc_i[1, span, :] += dy * x
        dz_ref[span, :] = (dgated * y * (sg + sgate * (1.0 - sg))).astype(BF16)

        gap = cum[one, :] - cum_t[:, one]
        decay = jnp.exp(jnp.where(seen, gap, -1e30))
        mixing = (scores * decay).astype(BF16)
        dyb = dy.astype(BF16)
        xd = x * step[one, :]
        xdb = xd.astype(BF16)
        dscores = dscores + dot_tn(xdb, dyb) * decay
        dstb = dstate[span, :].astype(BF16)
        dxd = dot_nt(dyb, mixing) + to_end[one, :] * dot_nn(dstb, key)
        wxd = (xd * to_end[one, :]).astype(BF16)
        edy = (dy * grown[one, :]).astype(BF16)
        dkey = dkey + dot_tn(dstb, wxd)
        dquery = dquery + dot_tn(s_ref[0, span, :].astype(BF16), edy)
        prod[0, one, :] = jnp.sum(
            dyb.astype(F32) * scan - xdb.astype(F32) * dxd, axis=0, keepdims=True
        )
        prod[1, one, :] = jnp.sum(x * dxd, axis=0, keepdims=True)
        held = dstate[span, :]
        prod[2, one, :] = jnp.sum(snext[span, :] * held, axis=0, keepdims=True)
        dstate[span, :] = fade[one, :] * held + dot_nt(edy, query)
        dact[span, :] = step[one, :] * dxd + row_ref[span, 1:2] * dy
    snext[...] = s_ref[0]
    dsb = dscores.astype(BF16)
    dact[inner : inner + states, :] = dkey + dot_nt(query, dsb)
    dact[inner + states :, :] = dquery + dot_nn(key, dsb)

    live = rows_of((hrows, CHUNK)) < heads
    lower = (rows_of((CHUNK, CHUNK)) >= lanes_of((CHUNK, CHUNK))).astype(F32)
    zero = jnp.zeros((hrows, CHUNK), F32)
    dla = lax.dot_general(
        jnp.where(live, prod[0], zero), lower, (((1,), (0,)), ((), ())), precision=HIGH,
        preferred_element_type=F32,
    ) + jnp.sum(jnp.where(live, prod[2], zero), axis=1, keepdims=True)
    dstep = jnp.where(live, prod[1], zero) + rate * dla
    draw = dstep * sigmoid(raw)
    acc_h[0] += draw
    acc_h[1] += step * dla
    dz_ref[inner + chans :, :] = draw.astype(BF16)

    for row in range(0, chans, width):
        span = slice(row, row + width)
        dconv = dact[span, :] * slope[span, :]
        acc_c[TAPS, span, :] += dconv
        acc_c[TAPS - 1, span, :] += dconv * z_ref[inner + row : inner + row + width, :].astype(F32)
        back = wide[TAPS - 1, span, :] * dconv
        after = later[span, :]
        for by in range(1, TAPS):
            acc_c[TAPS - 1 - by, span, :] += dconv * shifts[by - 1, span, :]
            back = back + wide[TAPS - 1 - by, span, :] * shifted_left(dconv, after, by)
        later[span, :] = dconv
        dz_ref[inner + row : inner + row + width, :] = back.astype(BF16)

    @pl.when(at == total - 1)
    def _():
        ones = jnp.ones((8, CHUNK), F32)

        def sums(block):
            return lax.dot_general(
                ones, block, (((1,), (1,)), ((), ())), precision=HIGH, preferred_element_type=F32
            )

        for which in range(TAPS + 1):
            chan_ref[which] = sums(acc_c[which])
        for which in range(2):
            inner_ref[which] = sums(acc_i[which])
            hsum_ref[which] = acc_h[which]


def backward_mix(z, dw, r, y, s, conv_cols, head_cols, row_cols, dims):
    inner, heads, width, states = dims
    chans = inner + 2 * states
    rows, length = z.shape
    hrows = head_cols.shape[0]
    count = length // CHUNK
    back = lambda c: (0, count - 1 - c)
    return pl.pallas_call(
        functools.partial(backward_body, dims),
        grid=(count,),
        in_specs=[
            pl.BlockSpec((rows, CHUNK), back),
            pl.BlockSpec((rows, CHUNK), lambda c: (0, jnp.maximum(count - 2 - c, 0))),
            pl.BlockSpec((inner, CHUNK), back),
            pl.BlockSpec((8, CHUNK), back),
            pl.BlockSpec((inner, CHUNK), back),
            pl.BlockSpec((1, inner, states), lambda c: (count - 1 - c, 0, 0)),
            pl.BlockSpec(conv_cols.shape, lambda c: (0, 0)),
            pl.BlockSpec(head_cols.shape, lambda c: (0, 0)),
            pl.BlockSpec(row_cols.shape, lambda c: (0, 0)),
        ],
        out_specs=[
            pl.BlockSpec((rows, CHUNK), back),
            pl.BlockSpec((TAPS + 1, 8, chans), lambda c: (0, 0, 0)),
            pl.BlockSpec((2, 8, inner), lambda c: (0, 0, 0)),
            pl.BlockSpec((2, hrows, CHUNK), lambda c: (0, 0, 0)),
        ],
        out_shape=[
            jax.ShapeDtypeStruct((rows, length), BF16),
            jax.ShapeDtypeStruct((TAPS + 1, 8, chans), F32),
            jax.ShapeDtypeStruct((2, 8, inner), F32),
            jax.ShapeDtypeStruct((2, hrows, CHUNK), F32),
        ],
        scratch_shapes=[
            pltpu.VMEM((chans, CHUNK), F32),
            pltpu.VMEM((chans, CHUNK), F32),
            pltpu.VMEM((TAPS - 1, chans, CHUNK), F32),
            pltpu.VMEM((chans, CHUNK), F32),
            pltpu.VMEM((inner, states), F32),
            pltpu.VMEM((inner, states), F32),
            pltpu.VMEM((chans, CHUNK), F32),
            pltpu.VMEM((TAPS + 1, chans, CHUNK), F32),
            pltpu.VMEM((TAPS + 1, chans, CHUNK), F32),
            pltpu.VMEM((2, inner, CHUNK), F32),
            pltpu.VMEM((2, hrows, CHUNK), F32),
            pltpu.VMEM((3, hrows, CHUNK), F32),
        ],
        cost_estimate=pl.CostEstimate(
            flops=4 * length * inner * (CHUNK + 2 * states) * 2,
            bytes_accessed=rows * length * 6 + inner * length * 6 + count * inner * states * 4,
            transcendentals=length * heads * CHUNK,
        ),
        name="mix_backward",
    )(z, z, dw, r, y, s, conv_cols, head_cols, row_cols)


SMALLS = 9


def per_device(
    block_input,
    zx_weight,
    bc_weight,
    dt_weight,
    out_weight,
    norm_gain,
    inner_conv,
    inner_conv_bias,
    state_conv,
    state_conv_bias,
    dt_bias,
    a_log,
    d_skip,
    gated_gain,
    cotangent,
):
    layers, _, shard, inner = zx_weight.shape
    sequences, length, model = block_input.shape
    pair = bc_weight.shape[2]
    states = pair // 2
    heads = dt_weight.shape[2]
    width = inner // heads
    inner_total = inner * lax.axis_size("mp")
    hrows = -(-heads // 16) * 16
    chans = inner + pair
    dims = (inner, heads, width, states)

    in_full, out_full, cols = [], [], []
    for layer in range(layers):
        packed = jnp.concatenate(
            [
                zx_weight[layer, 0],
                zx_weight[layer, 1],
                bc_weight[layer],
                jnp.pad(dt_weight[layer], ((0, 0), (0, hrows - heads))),
            ],
            axis=1,
        )
        in_full.append(lax.all_gather(packed, "dp", axis=0, tiled=True))
        out_full.append(lax.all_gather(out_weight[layer].T, "dp", axis=0, tiled=True))
        taps = jnp.concatenate([inner_conv[layer], state_conv[layer]], axis=1)
        offset = jnp.concatenate([inner_conv_bias[layer], state_conv_bias[layer]])
        conv_cols = jnp.pad(jnp.concatenate([taps, offset[None]], axis=0), ((0, 3), (0, 0))).T
        head_cols = jnp.pad(
            jnp.stack([dt_bias[layer], -jnp.exp(a_log[layer])], axis=1),
            ((0, hrows - heads), (0, 6)),
        )
        row_cols = jnp.pad(
            jnp.stack([gated_gain[layer], jnp.repeat(d_skip[layer], width)], axis=1),
            ((0, 0), (0, 6)),
        )
        cols.append((conv_cols, head_cols, row_cols))

    def forward_layer(layer, hidden):
        root = lax.rsqrt(jnp.mean(hidden * hidden, axis=-1) + EPS)
        normed = (hidden * root[:, None] * norm_gain[layer][None, :]).astype(BF16)
        z = jnp.einsum("df,td->ft", in_full[layer], normed, preferred_element_type=F32).astype(BF16)
        weighted, squares, scan, held = forward_mix(z, *cols[layer], dims)
        partial = jnp.einsum(
            "it,di->td", weighted, out_full[layer], preferred_element_type=F32
        ).astype(BF16)
        summed = lax.psum(partial, "mp").astype(F32)
        scale = lax.rsqrt(lax.psum(jnp.sum(squares, axis=0), "mp") / inner_total + EPS)
        kept = (hidden, root, normed, z, weighted, scan, held, scale, summed)
        return hidden + scale[:, None] * summed, kept

    def backward_layer(layer, kept, grad):
        hidden, root, normed, z, weighted, scan, held, scale, summed = kept
        dsummed = (scale[:, None] * grad).astype(BF16)
        dscale = jnp.sum(grad * summed, axis=-1)
        ratio = dscale * scale**3 / inner_total
        dweighted = jnp.einsum(
            "td,di->it", dsummed, out_full[layer], preferred_element_type=F32
        ).astype(BF16)
        dz, dchan, dinner, dheads = backward_mix(
            z, dweighted, jnp.broadcast_to(ratio, (8, length)), scan, held, *cols[layer], dims
        )
        partial = jnp.einsum("ft,df->td", dz, in_full[layer], preferred_element_type=F32).astype(
            BF16
        )
        dnormed = lax.psum(partial, "mp").astype(F32)
        unit = hidden * root[:, None]
        dnorm = jnp.sum(dnormed * unit, axis=0)
        back = dnormed * norm_gain[layer][None, :]
        grad = grad + root[:, None] * (
            back - unit * jnp.mean(back * unit, axis=-1, keepdims=True)
        )
        return grad, (normed, dz, dsummed, weighted), (dnorm, dchan, dinner, dheads)

    hidden = [block_input[seq].astype(F32) for seq in range(sequences)]
    kept = [[None] * sequences for _ in range(layers)]
    for layer in range(layers):
        for seq in range(sequences):
            hidden[seq], kept[layer][seq] = forward_layer(layer, hidden[seq])
    outputs = jnp.stack([item.astype(BF16) for item in hidden])

    grad = [cotangent[seq].astype(F32) for seq in range(sequences)]
    in_grads, out_grads, small_grads = [None] * layers, [None] * layers, [None] * layers
    for layer in reversed(range(layers)):
        bigs, smalls = [], []
        for seq in range(sequences):
            grad[seq], big, small = backward_layer(layer, kept[layer][seq], grad[seq])
            bigs.append(big)
            smalls.append(small)
        out_term = sum(
            jnp.einsum("td,it->di", big[2], big[3], preferred_element_type=F32) for big in bigs
        )
        in_term = sum(
            jnp.einsum("td,ft->df", big[0], big[1], preferred_element_type=F32) for big in bigs
        )
        out_grads[layer] = lax.psum_scatter(
            out_term.astype(BF16), "dp", scatter_dimension=0, tiled=True
        )
        in_grads[layer] = lax.psum_scatter(
            in_term.astype(BF16), "dp", scatter_dimension=0, tiled=True
        )
        small_grads[layer] = [sum(parts) for parts in zip(*smalls)]
    input_grad = jnp.stack(grad)

    out_grad = jnp.stack([item.T for item in out_grads]).astype(F32)
    in_grad = jnp.stack(in_grads)
    zx_grad = jnp.stack([in_grad[:, :, :inner], in_grad[:, :, inner : 2 * inner]], axis=1)
    zx_grad = zx_grad.astype(F32)
    dt_grad = in_grad[:, :, 2 * inner + pair : 2 * inner + pair + heads].astype(F32)
    bc_part = in_grad[:, :, 2 * inner : 2 * inner + pair]

    dnorm = jnp.stack([item[0] for item in small_grads])
    dchan = jnp.stack([item[1][:, 0] for item in small_grads])
    dinner = jnp.stack([item[2][:, 0] for item in small_grads])
    dheads = jnp.stack([jnp.sum(item[3], axis=-1)[:, :heads] for item in small_grads])
    dskip = jnp.sum(dinner[:, 1].reshape(layers, heads, width), axis=-1)
    dlog = dheads[:, 1] * -jnp.exp(a_log)
    vector = jnp.concatenate(
        [dnorm, dchan.reshape(layers, -1), dinner[:, 0], dheads[:, 0], dlog, dskip], axis=1
    )
    vector = lax.psum(vector, "dp")
    spots = [model, model + (TAPS + 1) * chans]
    spots += [spots[1] + inner]
    spots += [spots[2] + heads, spots[2] + 2 * heads]
    dnorm, dchan, dgain, dbias, dlog, dskip = jnp.split(vector, spots, axis=1)
    dchan = dchan.reshape(layers, TAPS + 1, chans)
    shared = lax.psum(
        jnp.concatenate(
            [bc_part.reshape(-1).astype(F32), dchan[:, :, inner:].reshape(-1)]
        ).astype(BF16),
        "mp",
    ).astype(F32)
    cut = bc_part.size
    bc_grad = shared[:cut].reshape(bc_part.shape)
    dstate = shared[cut:].reshape(layers, TAPS + 1, pair)
    return (
        outputs,
        input_grad,
        zx_grad,
        bc_grad,
        dt_grad,
        out_grad,
        dnorm,
        dchan[:, :TAPS, :inner],
        dchan[:, TAPS, :inner],
        dstate[:, :TAPS],
        dstate[:, TAPS],
        dbias,
        dlog,
        dskip,
        dgain,
    )


def solution(mesh):
    placed = (
        P("dp", None, None),
        P(None, None, "dp", "mp"),
        P(None, "dp", None),
        P(None, "dp", "mp"),
        P(None, "mp", "dp"),
        P(),
        P(None, None, "mp"),
        P(None, "mp"),
        P(),
        P(),
        P(None, "mp"),
        P(None, "mp"),
        P(None, "mp"),
        P(None, "mp"),
        P("dp", None, None),
    )
    return jax.shard_map(
        per_device,
        mesh=mesh,
        in_specs=placed,
        out_specs=(
            P("dp", None, None),
            P("dp", None, None),
            P(None, None, "dp", "mp"),
            P(None, "dp", None),
            P(None, "dp", "mp"),
            P(None, "mp", "dp"),
            P(),
            P(None, None, "mp"),
            P(None, "mp"),
            P(),
            P(),
            P(None, "mp"),
            P(None, "mp"),
            P(None, "mp"),
            P(None, "mp"),
        ),
        check_vma=False,
    )
```

time: 2900 us -> 1470 us (0.51)
  matrix products: 749 us -> 219 us
  local copies, waits for them, and re-layouts: 556 us -> 28 us
  other arithmetic: 442 us -> 85.5 us
  blocking collectives: 337 us -> 50.9 us
  Pallas kernels: 0 us -> 179 us
  waiting for transfers between devices: 762 us -> 884 us
    dot_general x272 -> x24, matrix products: 749 us -> 219 us  [the longest x4 50.1 us: per_device(): jnp.einsum('td,ft->df', big[0], big[1], preferred_element_type=F32)]
    all_gather x8 -> x0, blocking collectives: 274 us -> none  [the longest x4 139 us: gather_layer(): lax.all_gather(bc_weight[layer_at], 'dp', axis=0, tiled=True)]
    pallas_call x0 -> x8, Pallas kernels: none -> 179 us  [the longest x4 121 us: backward_mix(): pl.pallas_call(functools.partial(backward_body, dims), grid=(count,), in_...]
    another operation x272 -> x11, local copies, waits for them, and re-layouts: 122 us -> 0.82 us  [the longest x5 0.54 us: per_device(): jnp.stack([gated_gain[layer], jnp.repeat(d_skip[layer], width)], axis=1)]
    psum x9 -> x5, waiting for transfers between devices: 293 us -> 400 us  [the longest x2 219 us: forward_layer(): summed = lax.psum(partial, 'mp').astype(F32)]
    another operation x207 -> x13, other arithmetic: 130 us -> 31.1 us  [the longest x2 21.5 us: per_device(): input_grad = jnp.stack(grad)]
    reduce_sum x64 -> x0, local copies, waits for them, and re-layouts: 83 us -> none  [the longest x32 47.2 us: one_block(): gaps = log_decay[:, None, :] - log_decay[None, :, :]]
    reduce_sum x64 -> x13, other arithmetic: 127 us -> 46.6 us  [the longest x2 19.5 us: backward_layer(): dnorm = jnp.sum(dnormed * unit, axis=0)]
  transfers between devices with their start and end apart: 21 -> 13, of which waited for: 14 -> 11; matrix products, arithmetic and copies ran while one was open for 19% -> 13% of each run, Pallas kernels for 0% -> 4%
where the time goes in v1:
time: 1470 us; the launch traced here: 1460 us
  waiting for transfers between devices  884 us (60%)
  matrix products  219 us (15%)
  Pallas kernels  179 us (12%)
  other arithmetic  85.5 us (6%)
  blocking collectives  50.9 us (3%)
  local copies, waits for them, and re-layouts  28 us (2%)
  between operations  15 us (1%)
    reduce_scatter x2, waiting for transfers between devices, per_device(): lax.psum_scatter(in_term.astype(BF16), 'dp', scatter_dimension=0, tiled=T...  229 us
    psum x2, waiting for transfers between devices, forward_layer(): summed = lax.psum(partial, 'mp').astype(F32)  219 us
    all_gather x2, waiting for transfers between devices, per_device(): in_full.append(lax.all_gather(packed, 'dp', axis=0, tiled=True))  179 us
    psum x2, waiting for transfers between devices, backward_layer(): dnormed = lax.psum(partial, 'mp').astype(F32)  152 us
    pallas_call x4, Pallas kernels, backward_mix(): pl.pallas_call(functools.partial(backward_body, dims), grid=(count,), in_...  121 us
    reduce_scatter x2, waiting for transfers between devices, per_device(): lax.psum_scatter(out_term.astype(BF16), 'dp', scatter_dimension=0, tiled=...  76.8 us
    pallas_call x4, Pallas kernels, forward_mix(): pl.pallas_call(functools.partial(forward_body, dims), grid=(count,), in_s...  58 us
    dot_general x4, matrix products, per_device(): jnp.einsum('td,ft->df', big[0], big[1], preferred_element_type=F32)  50.1 us
  transfers between devices with their start and end apart: 13, of which 11 were waited for; matrix products, arithmetic and copies ran while one was open for 13% of the time, Pallas kernels for 4%

profile of v1, /device:TPU:0, one launch (start us, length us, event | category | flops | bytes accessed | tf_op | source)
XLA Modules:
  0.0 1463.0 jit_solution(13160705945320759956)
XLA Ops:
  9.2 1.3 slice_bitcast_fusion.5
  11.5 1.9 slice_bitcast_fusion
  14.1 3.5 fusion.35
  20.5 87.8 %all-gather.5.cloned.1.call-done = bf16[1536,1808]{1,0:T(8,128)(2,1)} async-done(((bf16[192,1808]{1,0:T(8,128)(2,1)}), bf16[1536,1808]{1,0:T(8,128)(2,1)}) %all-gather.5.cloned.1.call-update) | async-done | bytes 5554192 | tf_op jit(solution)/shard_map/all_gather | solution.py:403
  108.3 11.6 convolution_convert_fusion.11.z_ref.zp_ref
  119.9 14.5 mix_forward.4
  134.4 12.0 convolution_convert_fusion.7.z_ref.zp_ref
  146.4 14.5 mix_forward.6
  160.9 19.7 %convolution_convert_fusion.10 = bf16[1024,1536]{1,0:T(8,128)(2,1)} fusion(bf16[768,1024]{1,0:T(8,128)(2,1)S(1)} %copy-done.43, bf16[1536,768]{1,0:T(8,128)(2,1)} %all-gather.7.cloned.1.call-done), kind=kOutput, calls=%fused_computation.90 | convolution fusion | flops 2417491968 | bytes 7077888 | tf_op jit(solution)/shard_map/it,di->td/dot_general | solution.py:423
  180.6 4.1 convolution_convert_fusion.6
  189.3 6.8 all-reduce.9
  196.1 107.2 %all-reduce.28.cloned.1.call-done = (bf16[1024,1536]{1,0:T(8,128)(2,1)}, bf16[1024,1536]{1,0:T(8,128)(2,1)}) async-done(((bf16[1024,1536]{1,0:T(8,128)(2,1)}, bf16[1024,1536]{1,0:T(8,128)(2,1)}), (bf16[1024,1536]{1,0:T(8,128)(2,1)}, bf16[1024,1536]{1,0:T(8,128)(2,1)})) %all-reduce.28.cloned.1.call-update) | async-done | bytes 6291472 | tf_op jit(solution)/shard_map/psum | solution.py:426
  303.3 6.0 multiply_reduce_fusion.1
  309.4 90.7 %all-gather.9.cloned.1.call-done = bf16[1536,1808]{1,0:T(8,128)(2,1)} async-done(((bf16[192,1808]{1,0:T(8,128)(2,1)}), bf16[1536,1808]{1,0:T(8,128)(2,1)}) %all-gather.9.cloned.1.call-update) | async-done | bytes 5554192 | tf_op jit(solution)/shard_map/all_gather | solution.py:403
  400.1 12.1 convolution_convert_fusion.9.z_ref.zp_ref
  412.2 14.5 mix_forward.5
  426.7 11.8 convolution_convert_fusion.5.z_ref.zp_ref
  438.5 14.5 mix_forward.7
  453.1 6.6 convolution_convert_fusion.8
  459.7 4.1 convolution_convert_fusion.4
  464.6 5.8 all-reduce.8
  470.4 111.4 %all-reduce.26.cloned.1.call-done = (bf16[1024,1536]{1,0:T(8,128)(2,1)}, bf16[1024,1536]{1,0:T(8,128)(2,1)}) async-done(((bf16[1024,1536]{1,0:T(8,128)(2,1)}, bf16[1024,1536]{1,0:T(8,128)(2,1)}), (bf16[1024,1536]{1,0:T(8,128)(2,1)}, bf16[1024,1536]{1,0:T(8,128)(2,1)})) %all-reduce.26.cloned.1.call-update) | async-done | bytes 6291472 | tf_op jit(solution)/shard_map/psum | solution.py:426
  581.8 6.1 fusion.41
  588.4 4.3 fusion.48.dw_ref
  593.3 30.0 %mix_backward.6 = (bf16[1808,1024]{1,0:T(8,128)(2,1)}, f32[5,8,1024]{2,1,0:T(8,128)}, f32[2,8,768]{2,1,0:T(8,128)}, f32[2,16,128]{2,1,0:T(8,128)}) custom-call(bf16[1808,1024]{1,0:T(8,128)(2,1)} %convolution_convert_fusion.5.z_ref.zp_ref, bf16[1808,1024]{1,0:T(8,128)(2,1)} %convolution_convert_fusion.5.z_ref.zp_ref, bf16[768,1024]{1,0:T(8,128)(2,1)} %fusion.48.dw_ref, ...), custom_call_target="tpu_custom_call" | custom-call | flops 2415919104 | bytes 18972672 | tf_op jit(solution)/shard_map/mix_backward/pallas_call | solution.py:312
  623.3 6.6 fusion.46.dw_ref
  630.6 30.2 %mix_backward.4 = (bf16[1808,1024]{1,0:T(8,128)(2,1)}, f32[5,8,1024]{2,1,0:T(8,128)}, f32[2,8,768]{2,1,0:T(8,128)}, f32[2,16,128]{2,1,0:T(8,128)}) custom-call(bf16[1808,1024]{1,0:T(8,128)(2,1)} %convolution_convert_fusion.9.z_ref.zp_ref, bf16[1808,1024]{1,0:T(8,128)(2,1)} %convolution_convert_fusion.9.z_ref.zp_ref, bf16[768,1024]{1,0:T(8,128)(2,1)} %fusion.46.dw_ref, ...), custom_call_target="tpu_custom_call" | custom-call | flops 2415919104 | bytes 18972672 | tf_op jit(solution)/shard_map/mix_backward/pallas_call | solution.py:312
  660.8 11.2 convolution_convert_fusion.1
  672.1 8.4 convolution_convert_fusion.3
  680.6 119.9 %all-reduce.24.cloned.1.call-done = (bf16[1024,1536]{1,0:T(8,128)(2,1)}, bf16[1024,1536]{1,0:T(8,128)(2,1)}) async-done(((bf16[1024,1536]{1,0:T(8,128)(2,1)}, bf16[1024,1536]{1,0:T(8,128)(2,1)}), (bf16[1024,1536]{1,0:T(8,128)(2,1)}, bf16[1024,1536]{1,0:T(8,128)(2,1)})) %all-reduce.24.cloned.1.call-update) | async-done | bytes 6291472 | tf_op jit(solution)/shard_map/psum | solution.py:445
  800.6 12.6 fusion.30
  814.9 11.1 fusion.24
  826.0 4.3 fusion.47.dw_ref
  831.0 30.4 %mix_backward.5 = (bf16[1808,1024]{1,0:T(8,128)(2,1)}, f32[5,8,1024]{2,1,0:T(8,128)}, f32[2,8,768]{2,1,0:T(8,128)}, f32[2,16,128]{2,1,0:T(8,128)}) custom-call(bf16[1808,1024]{1,0:T(8,128)(2,1)} %convolution_convert_fusion.11.z_ref.zp_ref, bf16[1808,1024]{1,0:T(8,128)(2,1)} %convolution_convert_fusion.11.z_ref.zp_ref, bf16[768,1024]{1,0:T(8,128)(2,1)} %fusion.47.dw_ref, ...), custom_call_target="tpu_custom_call" | custom-call | flops 2415919104 | bytes 18972672 | tf_op jit(solution)/shard_map/mix_backward/pallas_call | solution.py:312
  861.4 7.6 fusion.49.dw_ref
  869.6 30.1 %mix_backward.7 = (bf16[1808,1024]{1,0:T(8,128)(2,1)}, f32[5,8,1024]{2,1,0:T(8,128)}, f32[2,8,768]{2,1,0:T(8,128)}, f32[2,16,128]{2,1,0:T(8,128)}) custom-call(bf16[1808,1024]{1,0:T(8,128)(2,1)} %convolution_convert_fusion.7.z_ref.zp_ref, bf16[1808,1024]{1,0:T(8,128)(2,1)} %convolution_convert_fusion.7.z_ref.zp_ref, bf16[768,1024]{1,0:T(8,128)(2,1)} %fusion.49.dw_ref, ...), custom_call_target="tpu_custom_call" | custom-call | flops 2415919104 | bytes 18972672 | tf_op jit(solution)/shard_map/mix_backward/pallas_call | solution.py:312
  899.7 11.3 convolution_convert_fusion.2
  911.1 8.4 convolution_convert_fusion
  919.5 1.3 copy-done.47
  920.9 5.0 fusion.54
  925.9 6.8 add_convert_fusion.2
  932.7 5.7 fusion.83
  938.4 7.4 add_convert_fusion.3
  946.0 13.7 fusion.84
  959.7 13.7 add_convert_fusion
  974.1 10.4 fusion.65
  984.6 12.2 add_convert_fusion.1
  997.6 1.1 fusion.72
  998.6 1.0 slice_add_fusion
  1000.9 1.0 slice_add_fusion.1
  1001.9 5.3 pad_maximum_fusion.1
  1007.2 32.3 %all-reduce.22.cloned.1.call-done = (bf16[1024,1536]{1,0:T(8,128)(2,1)}, bf16[1024,1536]{1,0:T(8,128)(2,1)}) async-done(((bf16[1024,1536]{1,0:T(8,128)(2,1)}, bf16[1024,1536]{1,0:T(8,128)(2,1)}), (bf16[1024,1536]{1,0:T(8,128)(2,1)}, bf16[1024,1536]{1,0:T(8,128)(2,1)})) %all-reduce.22.cloned.1.call-update) | async-done | bytes 6291472 | tf_op jit(solution)/shard_map/psum | solution.py:445
  1039.5 6.9 fusion.34
  1046.5 38.3 %psum.110 = f32[2,7460]{1,0:T(2,128)S(1)} all-reduce(f32[2,7460]{1,0:T(2,128)S(1)} %concatenate.40), channel_id=1, replica_groups=mesh['dp'=8,'mp'=4] {'dp'}, use_global_device_ids=true, to_apply=%region_37.38 | all-reduce | flops 14920 | bytes 119360 | tf_op jit(solution)/shard_map/psum | solution.py:500
  1088.0 12.7 fusion.21
  1100.7 8.8 pad_maximum_fusion
  1109.5 4.6 reduce-scatter.11.cloned.1.call-done
  1114.1 72.2 %reduce-scatter.9.cloned.1.call-done = bf16[192,768]{1,0:T(8,128)(2,1)} async-done(((bf16[1536,768]{1,0:T(8,128)(2,1)}), bf16[192,768]{1,0:T(8,128)(2,1)}) %reduce-scatter.9.cloned.1.call-update) | async-done | bytes 294928 | tf_op jit(solution)/shard_map/reduce_scatter | solution.py:475
  1186.4 2.1 maximum_convert_fusion.1
  1188.5 113.2 %reduce-scatter.7.cloned.1.call-done = bf16[192,1808]{1,0:T(8,128)(2,1)} async-done(((bf16[1536,1808]{1,0:T(8,128)(2,1)}), bf16[192,1808]{1,0:T(8,128)(2,1)}) %reduce-scatter.7.cloned.1.call-update) | async-done | bytes 694288 | tf_op jit(solution)/shard_map/reduce_scatter | solution.py:478
  1301.7 115.3 %reduce-scatter.5.cloned.1.call-done = bf16[192,1808]{1,0:T(8,128)(2,1)} async-done(((bf16[1536,1808]{1,0:T(8,128)(2,1)}), bf16[192,1808]{1,0:T(8,128)(2,1)}) %reduce-scatter.5.cloned.1.call-update) | async-done | bytes 694288 | tf_op jit(solution)/shard_map/reduce_scatter | solution.py:478
  1418.9 1.3 fusion.60
  1422.0 1.6 copy.86
  1423.5 29.0 %all-reduce.20.cloned.1.call-done = bf16[100864]{0:T(1024)(128)(2,1)} async-done(((bf16[100864]{0:T(1024)(128)(2,1)}), bf16[100864]{0:T(1024)(128)(2,1)}) %all-reduce.20.cloned.1.call-update) | async-done | bytes 201744 | tf_op jit(solution)/shard_map/psum | solution.py:506
  (244 shorter events, 29.6 us)
Async XLA Ops:
  7.2 6.3 copy-start.33
  7.2 6.3 copy-start.34
  7.2 6.4 copy-start.30
  7.2 6.4 copy-start.32
  7.2 6.4 copy-start.29
  7.2 6.8 copy-start.28
  7.2 6.8 copy-start.27
  7.3 101.0 %all-gather.5.cloned.1.call-start = ((), (), s32[]{:S(2)}) async-start(), calls=%async_computation.4 | async-start | bytes 6635520 | tf_op jit(solution)/shard_map/all_gather | solution.py:403
  9.2 8.4 copy-start.26
  9.2 8.5 copy-start.21
  11.5 149.4 %all-gather.7.cloned.1.call-start = ((), (), s32[]{:S(2)}) async-start(), calls=%async_computation.5 | async-start | bytes 2654208 | tf_op jit(solution)/shard_map/all_gather | solution.py:404
  13.5 289.8 %all-reduce.28.cloned.1.call-start = ((), (), s32[]{:S(2)}) async-start(), calls=%async_computation.16 | async-start | bytes 12582912 | tf_op jit(solution)/shard_map/psum | solution.py:426
  17.7 116.7 %copy-start.9 = (f32[1536]{0:T(1024)}, f32[1536]{0:T(1024)S(1)}, u32[]{:S(2)}) copy-start(f32[1536]{0:T(1024)S(1)} %get-tuple-element.143) | copy-start | bytes 18436
  20.4 99.4 %copy-start.13 = (f32[1024]{0:T(1024)}, f32[1024]{0:T(1024)S(1)}, u32[]{:S(2)}) copy-start(f32[1024]{0:T(1024)S(1)} %get-tuple-element.206) | copy-start | bytes 12292
  20.4 113.9 %copy-start.11 = (f32[1024]{0:T(1024)}, f32[1024]{0:T(1024)S(1)}, u32[]{:S(2)}) copy-start(f32[1024]{0:T(1024)S(1)} %get-tuple-element.205) | copy-start | bytes 12292
  134.4 26.5 %copy-start.43 = (bf16[768,1024]{1,0:T(8,128)(2,1)S(1)}, bf16[768,1024]{1,0:T(8,128)(2,1)}, u32[]{:S(2)}) copy-start(bf16[768,1024]{1,0:T(8,128)(2,1)} %get-tuple-element.48) | copy-start | bytes 4718596
  160.9 19.7 %copy-start.39 = (bf16[1536,768]{1,0:T(8,128)(2,1)S(1)}, bf16[1536,768]{1,0:T(8,128)(2,1)}, u32[]{:S(2)}) copy-start(bf16[1536,768]{1,0:T(8,128)(2,1)} %all-gather.7.cloned.1.call-done) | copy-start | bytes 7077892
  160.9 19.7 %copy-start.45 = (bf16[768,1024]{1,0:T(8,128)(2,1)S(1)}, bf16[768,1024]{1,0:T(8,128)(2,1)}, u32[]{:S(2)}) copy-start(bf16[768,1024]{1,0:T(8,128)(2,1)} %get-tuple-element.52) | copy-start | bytes 4718596
  184.7 4.6 copy-start.17
  184.7 4.6 copy-start.18
  184.7 215.3 %all-gather.9.cloned.1.call-start = ((), (), s32[]{:S(2)}) async-start(), calls=%async_computation.6 | async-start | bytes 6635520 | tf_op jit(solution)/shard_map/all_gather | solution.py:403
  185.9 267.2 %all-gather.11.cloned.1.call-start = ((), (), s32[]{:S(2)}) async-start(), calls=%async_computation.7 | async-start | bytes 2654208 | tf_op jit(solution)/shard_map/all_gather | solution.py:404
  186.5 395.3 %all-reduce.26.cloned.1.call-start = ((), (), s32[]{:S(2)}) async-start(), calls=%async_computation.15 | async-start | bytes 12582912 | tf_op jit(solution)/shard_map/psum | solution.py:426
  400.1 26.6 %copy-start = (bf16[1024,1536]{1,0:T(8,128)(2,1)S(1)}, bf16[1024,1536]{1,0:T(8,128)(2,1)}, u32[]{:S(2)}) copy-start(bf16[1024,1536]{1,0:T(8,128)(2,1)} %get-tuple-element.157) | copy-start | bytes 9437188
  453.1 6.6 copy-start.41
  453.1 6.6 copy-start.48
  463.8 124.1 %slice-start.2 = ((s8[6291456]{0:T(1024)(128)(4,1)}), s8[2097152]{0:T(1024)(128)(4,1)S(1)}, s32[]{:S(2)}) async-start(s8[6291456]{0:T(1024)(128)(4,1)} %bitcast.212), calls=%async_computation.19 | async-start | bytes 4194304
  463.8 336.7 %all-reduce.24.cloned.1.call-start = ((), (), s32[]{:S(2)}) async-start(), calls=%async_computation.14 | async-start | bytes 12582912 | tf_op jit(solution)/shard_map/psum | solution.py:445
  581.8 6.2 slice-start.3
  581.8 6.6 copy-start.42
  630.6 41.5 %slice-start.6 = ((s8[5898240]{0:T(1024)(128)(4,1)}), s8[1703936]{0:T(1024)(128)(4,1)S(1)}, s32[]{:S(2)}) async-start(s8[5898240]{0:T(1024)(128)(4,1)} %bitcast.238), calls=%async_computation.23 | async-start | bytes 3407872
  660.8 11.3 slice-start.7
  660.8 11.3 copy-start.36
  680.5 132.7 %slice-start = ((s8[6291456]{0:T(1024)(128)(4,1)}), s8[2097152]{0:T(1024)(128)(4,1)S(1)}, s32[]{:S(2)}) async-start(s8[6291456]{0:T(1024)(128)(4,1)} %bitcast.210), calls=%async_computation.17 | async-start | bytes 4194304
  680.6 358.9 %all-reduce.22.cloned.1.call-start = ((), (), s32[]{:S(2)}) async-start(), calls=%async_computation.13 | async-start | bytes 12582912 | tf_op jit(solution)/shard_map/psum | solution.py:445
  800.6 12.7 slice-start.1
  800.6 12.7 copy-start.1
  800.6 12.7 copy-start.3
  800.6 12.7 copy-start.6
  800.6 13.4 copy-start.7
  800.6 14.3 copy-start.8
  814.9 11.1 copy-start.40
  826.0 4.4 copy-start.4
  869.6 41.4 %slice-start.4 = ((s8[5898240]{0:T(1024)(128)(4,1)}), s8[1703936]{0:T(1024)(128)(4,1)S(1)}, s32[]{:S(2)}) async-start(s8[5898240]{0:T(1024)(128)(4,1)} %bitcast.236), calls=%async_computation.21 | async-start | bytes 3407872
  899.7 11.3 slice-start.5
  899.7 11.3 copy-start.37
  919.5 194.6 %reduce-scatter.11.cloned.1.call-start = ((), (), s32[]{:S(2)}) async-start(), calls=%async_computation.12 | async-start | bytes 2654208 | tf_op jit(solution)/shard_map/reduce_scatter | solution.py:475
  920.9 5.0 copy-start.49
  925.9 6.9 copy-start.44
  932.7 5.7 copy-start.46
  932.7 253.7 %reduce-scatter.9.cloned.1.call-start = ((), (), s32[]{:S(2)}) async-start(), calls=%async_computation.11 | async-start | bytes 2654208 | tf_op jit(solution)/shard_map/reduce_scatter | solution.py:475
  945.9 13.8 copy-start.2
  945.9 355.9 %reduce-scatter.7.cloned.1.call-start = ((), (), s32[]{:S(2)}) async-start(), calls=%async_computation.9 | async-start | bytes 6635520 | tf_op jit(solution)/shard_map/reduce_scatter | solution.py:478
  945.9 13.8 copy-start.35
  973.4 11.1 copy-start.12
  973.4 443.6 %reduce-scatter.5.cloned.1.call-start = ((), (), s32[]{:S(2)}) async-start(), calls=%async_computation.8 | async-start | bytes 6635520 | tf_op jit(solution)/shard_map/reduce_scatter | solution.py:478
  974.1 10.5 copy-start.38
  996.8 2.9 copy-start.15
  996.8 2.9 copy-start.16
  996.8 4.0 copy-start.24
  996.8 4.0 copy-start.25
  996.8 4.0 copy-start.31
  996.8 5.1 copy-start.5
  996.8 455.7 %all-reduce.20.cloned.1.call-start = ((), (), s32[]{:S(2)}) async-start(), calls=%async_computation.10 | async-start | bytes 405504 | tf_op jit(solution)/shard_map/psum | solution.py:506
  (7 other events, 5.8 us)
Sparse Core Ops, SparseCore 0:
  11.6 96.6 all-gather.4
  111.0 49.8 all-gather.6
  184.9 118.4 all-reduce.27
  305.9 94.1 all-gather.8
  402.1 49.9 all-gather.10
  464.0 117.7 all-reduce.25
  680.7 119.8 all-reduce.23
  919.6 119.8 all-reduce.21
  1043.5 70.5 reduce-scatter.10
  1117.5 68.8 reduce-scatter.8
  1190.0 111.6 reduce-scatter.6
  1305.3 111.7 reduce-scatter.4
  1421.9 30.5 all-reduce.19
